TPU v7x, 32 devices: a whole 2x2x4 slice. The times are simulated.
32 devices in a mesh: dp: 8 (over y, x, core), seq: 4 (over z).
Axes of the slice: x: 2, y: 2, z: 4, core: 2. Of those that a mesh axis runs over, the one named last changes fastest.
Arguments:
- inputs: float32 [16, 768, 512], P('dp', 'seq'), may hold values from -6 to 6
- lengths: int32 [16], P('dp'), may hold values from 192 to 768, as said below
- rel_bucket: int32 [1535], replicated, may hold values from 0 to 31
- params: float32 [6059776], P(('dp', 'seq')), may hold values from -3 to 3, as said below
- moment_one: float32 [6059776], P(('dp', 'seq')), may hold values from -12288 to 12288
- moment_two: float32 [6059776], P(('dp', 'seq')), may hold values from 0 to 12288, as said below
- cotangent: float32 [16, 768, 512], P('dp', 'seq'), may hold values from -6 to 6
Outputs:
- block_output: float32 [16, 768, 512], P('dp', 'seq')
- input_grad: float32 [16, 768, 512], P('dp', 'seq')
- param_grad: float32 [6059776], P(('dp', 'seq'))
- new_params: float32 [6059776], P(('dp', 'seq'))
- new_moment_one: float32 [6059776], P(('dp', 'seq'))
- new_moment_two: float32 [6059776], P(('dp', 'seq'))
Inputs may be any that keep to these rules, and one draw needn't show every extreme that they name: `lengths`: some sequence is 768 tokens long in every draw. `params`: norm and batch-norm gains lie in 0.5 to 1.5. `moment_two`: every entry is positive.
All inputs are finite; a program needn't handle non-finite values.
Results may differ from a plain program's by a relative error of at most 0.012.
Values may be sent and summed in bfloat16 or wider, within the bound.
A program may use at most 256 MiB of HBM per device.

v0:
```python
import functools
import math

import jax
import jax.numpy as jnp
from jax import lax
from jax.experimental import pallas as pl
from jax.experimental.pallas import tpu as pltpu
from jax.sharding import PartitionSpec as P

D = 512
H = 8
HD = 64
FF = 2048
K = 31
NB = 32
DP = "dp"
SEQ = "seq"
STEP = 4


NORM_EPS = 1e-05
BATCH_EPS = 1e-05
LEARN_RATE = 0.005
DECAY = 0.01
BETA_ONE = 0.9
BETA_TWO = 0.98
ADAM_EPS = 1e-08


def with_halo(shard, sides, width):
    for axis, dim in sides:
        devices, length = (lax.axis_size(axis), shard.shape[dim])
        up = [(i, (i + 1) % devices) for i in range(devices - 1)]
        down = [(j, i) for i, j in up]
        last = lax.slice_in_dim(shard, length - width, length, axis=dim)
        leading = lax.slice_in_dim(shard, 0, width, axis=dim)
        before = lax.ppermute(last, axis, up)
        after = lax.ppermute(leading, axis, down)
        shard = jnp.concatenate([before, shard, after], axis=dim)
    return shard


def segments():

    def feed_block(prefix):
        return [
            (prefix + "_ng", (D,)),
            (prefix + "_nb", (D,)),
            (prefix + "_w_in", (D, FF)),
            (prefix + "_b_in", (FF,)),
            (prefix + "_w_out", (FF, D)),
            (prefix + "_b_out", (D,)),
        ]

    listing = feed_block("first")
    listing = listing + [
        ("attn_ng", (D,)),
        ("attn_nb", (D,)),
        ("w_q", (D, D)),
        ("b_q", (D,)),
        ("w_k", (D, D)),
        ("w_v", (D, D)),
        ("b_v", (D,)),
        ("w_o", (D, D)),
        ("b_o", (D,)),
        ("rel", (NB, H)),
    ]
    listing = listing + [
        ("conv_ng", (D,)),
        ("conv_nb", (D,)),
        ("w_pi", (D, 2 * D)),
        ("b_pi", (2 * D,)),
        ("w_depth", (K, D)),
        ("bng", (D,)),
        ("bnb", (D,)),
        ("w_po", (D, D)),
        ("b_po", (D,)),
    ]
    listing = listing + feed_block("second") + [("fin_g", (D,)), ("fin_b", (D,))]
    return listing


def arrange():
    places, gaps = {}, []
    linear = inner = 0
    for entry_name, entry_shape in segments():
        extent = math.prod(entry_shape)
        tail = 2 * D if entry_name == "conv_ng" else 0
        if extent >= D * D or tail:
            pad = -(inner + tail) % TILE
            if pad:
                gaps.append((linear, pad))
                inner = inner + pad
        places[entry_name] = inner // LANES
        linear, inner = linear + extent, inner + extent
    return places, gaps, -(-inner // TILE)


def unpack(rows):
    result = {}
    places = arrange()[0]
    for entry_name, entry_shape in segments():
        extent = math.prod(entry_shape)
        first = places[entry_name]
        piece = rows[first : first + -(-extent // LANES)]
        if extent < LANES:
            piece = piece[:, :extent]
        result[entry_name] = piece.reshape(entry_shape)
    return result


def device_index():
    return lax.axis_index(DP) * lax.axis_size(SEQ) + lax.axis_index(SEQ)


def own_block(plan, params):
    index = device_index()
    shift_down = [(i + 1, i) for i in range(plan.n - 1)]
    following = lax.ppermute(params[:TILE], (DP, SEQ), shift_down)
    length = plan.hi * TILE
    room = max(length + TILE - plan.shard - TILE, 0)
    front = max(size for _, size in plan.gaps)
    extended = jnp.concatenate(
        [jnp.zeros((front,), jnp.float32), params, following, jnp.zeros((room,), jnp.float32)]
    )
    table = jnp.asarray(plan.block_table, jnp.int32)[index]
    early = lax.dynamic_slice(extended, (front + table[0],), (length,))
    late = lax.dynamic_slice(extended, (front + table[0] - table[2],), (length,))
    block = jnp.where(jnp.arange(length, dtype=jnp.int32) < table[1], early, late)
    return block.astype(jnp.bfloat16).reshape(plan.hi, 8, LANES)


def own_shard(plan, window):
    table = jnp.asarray(plan.shard_table, jnp.int32)[device_index()]
    flat = window.reshape(-1)
    early = lax.dynamic_slice(flat, (table[0],), (plan.shard,))
    late = lax.dynamic_slice(flat, (table[0] + table[2],), (plan.shard,))
    return jnp.where(jnp.arange(plan.shard, dtype=jnp.int32) < table[1], early, late)


def vector(weights, entry_name):
    return weights[entry_name].astype(jnp.float32)


def swish_act(values):
    return values * jax.nn.sigmoid(values)


def swish_grad(values):
    sig_vals = jax.nn.sigmoid(values)
    return sig_vals * (1.0 + values * (1.0 - sig_vals))


def norm_rows(values, scale_vec, shift_vec):
    centre = values - jnp.mean(values, -1, keepdims=True)
    spread = jnp.mean(centre * centre, -1, keepdims=True)
    return centre * lax.rsqrt(spread + NORM_EPS) * scale_vec + shift_vec


def norm_back(values, scale_vec, shift_vec, grad_out):
    _, pullback = jax.vjp(norm_rows, values, scale_vec, shift_vec)
    return pullback(grad_out)


def forward_dot(left_mat, weight):
    return jnp.dot(left_mat, weight, preferred_element_type=jnp.float32)


def cross_dot(left_mat, right_mat):
    return lax.dot_general(
        left_mat, right_mat, (((0,), (0,)), ((), ())), preferred_element_type=jnp.float32
    )


def back_dot(grad_in, weight):
    return lax.dot_general(
        grad_in, weight, (((1,), (1,)), ((), ())), preferred_element_type=jnp.float32
    )


def ffn_forward(stream, weights, prefix):
    normed_b = norm_rows(
        stream, vector(weights, prefix + "_ng"), vector(weights, prefix + "_nb")
    ).astype(jnp.bfloat16)
    hidden = forward_dot(normed_b, weights[prefix + "_w_in"]) + vector(weights, prefix + "_b_in")
    active = swish_act(hidden).astype(jnp.bfloat16)
    output = stream + 0.5 * (
        forward_dot(active, weights[prefix + "_w_out"]) + vector(weights, prefix + "_b_out")
    )
    return (output, (normed_b, hidden, active))


def ffn_backward(stream, weights, prefix, stored, grad_out):
    normed_b, hidden, active = stored
    half_grad = 0.5 * grad_out
    half_b = half_grad.astype(jnp.bfloat16)
    gradients = {
        prefix + "_w_out": (active, half_b),
        prefix + "_b_out": jnp.sum(half_grad, 0),
    }
    d_hidden = back_dot(half_b, weights[prefix + "_w_out"]) * swish_grad(hidden)
    d_hidden_b = d_hidden.astype(jnp.bfloat16)
    gradients[prefix + "_w_in"] = (normed_b, d_hidden_b)
    gradients[prefix + "_b_in"] = jnp.sum(d_hidden, 0)
    d_normed = back_dot(d_hidden_b, weights[prefix + "_w_in"])
    d_stream, gain_grad, shift_grad = norm_back(
        stream,
        vector(weights, prefix + "_ng"),
        vector(weights, prefix + "_nb"),
        d_normed,
    )
    gradients[prefix + "_ng"] = gain_grad
    gradients[prefix + "_nb"] = shift_grad
    return (grad_out + d_stream, gradients)


MESH = pl.DeviceIdType.MESH
LANES=512
TILE=8*LANES

class Plan:
    def __init__(self, ndp, nseq, shard):
        self.ndp, self.nseq, self.shard = ndp, nseq, shard
        self.k = ndp.bit_length() - 1
        self.phases = self.k - 1
        self.n = n = ndp * nseq
        self.places, self.gaps, self.total = arrange()
        begins = [self.inner(d * shard) for d in range(n)]
        starts = [-(-b // TILE) for b in begins] + [self.total]
        sizes = [b - a for a, b in zip(starts, starts[1:])]
        self.lo, self.hi = min(sizes), max(sizes)
        self.slots = nseq * 2**self.phases
        floors = [b // TILE for b in begins]
        ends = [self.inner((d + 1) * shard - 1) // TILE + 1 for d in range(n)]
        self.win = max(e - f for e, f in zip(ends, floors))
        self.win += self.win % 2
        self.padded = max(self.total, max(floors) + self.win)
        self.block_table, self.shard_table = [], []
        for d in range(n):
            near = [g for g in self.gaps if d * shard < g[0] < (d + 1) * shard + TILE]
            assert len(near) <= 1
            cut, size = near[0] if near else (2**30, 0)
            lead = starts[d] * TILE - begins[d]
            self.block_table.append((lead, cut - d * shard - lead, size))
            self.shard_table.append((begins[d] - floors[d] * TILE, cut - d * shard, size))

    def inner(self, position):
        if isinstance(position, int):
            return position + sum(size for at, size in self.gaps if at <= position)
        result = position
        for at, size in self.gaps:
            result = result + jnp.where(position >= at, size, 0)
        return result

    def order(self):
        ev=[]
        for s in range(self.nseq):
            for sign in ((0,) if s==0 else (-1,1)):
                for t in range(2**self.phases):
                    ev.append((s+0.5*bin(t).count("1")+0.01*t, s, sign, t))
        ev.sort()
        return [e[1:] for e in ev]

def flip(di, mask_bits, bits, t, phases):
    out=di
    for p in range(phases):
        if (t>>p)&1:
            out = out + mask_bits[p]*(1-2*bits[p])
    return out

def phase_masks(di, c, phases):
    masks, bits=[],[]
    for p in range(phases):
        a, b = 1<<(p+1), 1<<(phases-p)
        masks.append(a+c*(b-a))
        ba, bb = (di//a)%2, (di//b)%2
        bits.append(ba+c*(bb-ba))
    return masks, bits

def block_of(plan, dpi, z):
    d = dpi*plan.nseq+z
    a = (plan.inner(d*plan.shard)+TILE-1)//TILE
    b = (plan.inner((d+1)*plan.shard)+TILE-1)//TILE
    b = jnp.where(d == plan.n-1, plan.total, b)
    return a, b-a

def floor_of(plan, dpi, z):
    return plan.inner((dpi*plan.nseq+z)*plan.shard)//TILE

def gather_kernel(plan, src, out, send_a, send_b, recv_a, recv_b, loc_sem):
    di, z = lax.axis_index(DP), lax.axis_index(SEQ)
    ns, ph = plan.nseq, plan.phases
    c = di%2
    masks, bits = phase_masks(di, c, ph)
    other = di+1-2*c
    omasks, obits = phase_masks(other, 1-c, ph)
    up, down = lax.rem(z+1,ns), lax.rem(z+ns-1,ns)
    partners=[(di,up),(di,down),(other,z)]+[(flip(di,masks,bits,1<<p,ph),z) for p in range(ph)]
    barrier=pltpu.get_barrier_semaphore()
    for a,b in partners:
        pl.semaphore_signal(barrier,inc=1,device_id=(a,b),device_id_type=MESH)
    pl.semaphore_wait(barrier,len(partners))
    lo, more = plan.lo, plan.hi-plan.lo
    start_own, size_own = block_of(plan, di, z)

    def pair(ref, base, dst_start, size, sidx, ridx, dev):
        copies=[pltpu.make_async_remote_copy(src_ref=ref.at[pl.ds(base,lo)],dst_ref=out.at[pl.ds(dst_start,lo)],
            send_sem=send_a.at[sidx],recv_sem=recv_a.at[ridx],device_id=dev,device_id_type=MESH)]
        for x in range(more):
            copies.append(pltpu.make_async_remote_copy(src_ref=ref.at[pl.ds(base+lo+x,1)],dst_ref=out.at[pl.ds(dst_start+lo+x,1)],
                send_sem=send_b.at[sidx*more+x],recv_sem=recv_b.at[ridx*more+x],device_id=dev,device_id_type=MESH))
        return copies, size
    def each(p, act):
        for x,copy in enumerate(p[0]):
            if x==0: act(copy)
            else:
                @pl.when(p[1]>=lo+x)
                def _(): act(copy)
    def start(p): each(p, lambda c: c.start())
    def wait_send(p): each(p, lambda c: c.wait_send())
    def wait_recv(p): each(p, lambda c: c.wait_recv())

    own=[pltpu.make_async_copy(src.at[pl.ds(0,lo)],out.at[pl.ds(start_own,lo)],loc_sem.at[0])]
    for x in range(more):
        own.append(pltpu.make_async_copy(src.at[pl.ds(lo+x,1)],out.at[pl.ds(start_own+lo+x,1)],loc_sem.at[1+x]))
    own=(own,size_own)
    start(own)
    nslot=plan.slots
    sends=[]
    sidx=[0]
    def forward(conds, ref, base, st, size, ridx, dev):
        i=sidx[0]; sidx[0]+=1
        p=pair(ref,base,st,size,i,ridx,dev)
        sends.append((conds,p))
        guard(conds, lambda: start(p))
    def guard(conds, fn):
        if not conds: fn(); return
        cond=conds[0]
        for x in conds[1:]: cond=jnp.logical_and(cond,x)
        @pl.when(cond)
        def _(): fn()

    for s, sign, t in plan.order():
        zz = z+sign*s
        conds=[] if s==0 else ([zz>=0] if sign<0 else [zz<ns])
        dpi=flip(di,masks,bits,t,ph)
        st,size=block_of(plan,dpi,zz)
        mine = s==0 and t==0
        ref, base = (src, 0) if mine else (out, st)
        slot = t*ns+zz
        if not mine:
            p=pair(out,st,st,size,0,slot,(di,z))
            guard(conds, lambda: wait_recv(p))
        if t==0:
            if sign<=0 : forward(conds+[z<ns-1],ref,base,st,size,slot,(di,z+1))
            if sign>=0 : forward(conds+[z>0],ref,base,st,size,slot,(di,z-1))
        hi_bit=t.bit_length()
        for pp in range(hi_bit,ph):
            forward(conds,ref,base,st,size,slot+(1<<pp)*ns,(flip(di,masks,bits,1<<pp,ph),z))
        forward(conds,ref,base,st,size,nslot+slot,(other,z))
    for s, sign, t in plan.order():
        zz=z+sign*s
        conds=[] if s==0 else ([zz>=0] if sign<0 else [zz<ns])
        dpi=flip(other,omasks,obits,t,ph)
        st,size=block_of(plan,dpi,zz)
        p=pair(out,st,st,size,0,nslot+t*ns+zz,(di,z))
        guard(conds,lambda: wait_recv(p))
    for conds,p in sends:
        guard(conds,lambda: wait_send(p))
    each(own, lambda c: c.wait())

def count_sends(plan):
    n=0
    for s,sign,t in plan.order():
        if t==0: n+= (2 if sign==0 else 1)
        n+=plan.phases-t.bit_length()+1
    return n

def gather(plan, block):
    ns=count_sends(plan)
    more=max(plan.hi-plan.lo,1)
    return pl.pallas_call(
        functools.partial(gather_kernel,plan),
        out_shape=jax.ShapeDtypeStruct((plan.total,8,LANES),block.dtype),
        in_specs=[pl.BlockSpec(memory_space=pl.ANY)],
        out_specs=pl.BlockSpec(memory_space=pl.ANY),
        scratch_shapes=[pltpu.SemaphoreType.DMA((ns,)),pltpu.SemaphoreType.DMA((ns*more,)),
            pltpu.SemaphoreType.DMA((2*plan.slots,)),pltpu.SemaphoreType.DMA((2*plan.slots*more,)),pltpu.SemaphoreType.DMA((1+more,))],
        compiler_params=pltpu.CompilerParams(collective_id=0,has_side_effects=True),
        name="gather_params",
    )(block)

def scatter_kernel(plan, g, out, acc, rc, rp, rz, load_sem, send_sem, core_send, core_recv, ph_recv, z_recv):
    di, z = lax.axis_index(DP), lax.axis_index(SEQ)
    ns, ph, win, nslot = plan.nseq, plan.phases, plan.win, plan.slots
    c = di%2
    masks, bits = phase_masks(di, c, ph)
    other = di+1-2*c
    omasks, obits = phase_masks(other, 1-c, ph)
    up, down = lax.rem(z+1,ns), lax.rem(z+ns-1,ns)
    partners=[(di,up),(di,down),(other,z)]+[(flip(di,masks,bits,1<<p,ph),z) for p in range(ph)]
    barrier=pltpu.get_barrier_semaphore()
    for a,b in partners:
        pl.semaphore_signal(barrier,inc=1,device_id=(a,b),device_id_type=MESH)
    order=list(reversed(plan.order()))
    def cond_of(s,sign):
        zz=z+sign*s
        return zz,([] if s==0 else ([zz>=0] if sign<0 else [zz<ns]))
    def guard(conds, fn):
        if not conds: fn(); return
        cond=conds[0]
        for x in conds[1:]: cond=jnp.logical_and(cond,x)
        @pl.when(cond)
        def _(): fn()
    def load(s,sign,t):
        zz,conds=cond_of(s,sign)
        slot=t*ns+zz
        st=floor_of(plan,flip(di,masks,bits,t,ph),zz)
        return conds,pltpu.make_async_copy(g.at[pl.ds(st,win)],acc.at[slot],load_sem.at[slot])
    def core(s,sign,t):
        zz,conds=cond_of(s,sign)
        slot=t*ns+zz
        st=floor_of(plan,flip(other,omasks,obits,t,ph),zz)
        return conds,pltpu.make_async_remote_copy(src_ref=g.at[pl.ds(st,win)],dst_ref=rc.at[slot],
            send_sem=core_send.at[slot],recv_sem=core_recv.at[slot],device_id=(other,z),device_id_type=MESH)
    for e in order:
        conds,cp=load(*e)
        guard(conds,lambda: cp.start())
    pl.semaphore_wait(barrier,len(partners))
    for e in order:
        conds,cp=core(*e)
        guard(conds,lambda: cp.start())
    sends=[]
    def send(conds,slot,dst,rsem,dev):
        i=len(sends)
        cp=pltpu.make_async_remote_copy(src_ref=acc.at[slot],dst_ref=dst,send_sem=send_sem.at[i],recv_sem=rsem,
            device_id=dev,device_id_type=MESH)
        sends.append((conds,cp))
        guard(conds,lambda: cp.start())
    def waiting(conds,dst,rsem):
        cp=pltpu.make_async_remote_copy(src_ref=dst,dst_ref=dst,send_sem=send_sem.at[0],recv_sem=rsem,
            device_id=(di,z),device_id_type=MESH)
        guard(conds,lambda: cp.wait_recv())
    step=2
    def add(dst, slot, parts, final=False):
        @pl.loop(0,win//step)
        def _(i):
            r=pl.ds(i*step,step)
            v=acc[slot,r].astype(jnp.float32)
            for p in parts:
                v=v+p(r).astype(jnp.float32)
            if final: out[r]=v
            else: acc[slot,r]=v.astype(acc.dtype)
    for s,sign,t in order:
        zz,conds=cond_of(s,sign)
        slot=t*ns+zz
        hi_bit=t.bit_length()
        def fn():
            load(s,sign,t)[1].wait()
            waiting([],rc.at[slot],core_recv.at[slot])
            parts=[lambda r: rc[slot,r]]
            for pp in range(hi_bit,ph):
                idx=((1<<pp)-1)*ns+slot
                waiting([],rp.at[idx],ph_recv.at[idx])
                parts.append(lambda r,idx=idx: rp[idx,r])
            add(None,slot,parts,final=False) if not (t==0 and s==0) else add(None,slot,parts,final=True)
        guard(conds,fn)
        if t:
            pp=hi_bit-1
            idx=((1<<pp)-1)*ns+slot-(1<<pp)*ns
            send(conds,slot,rp.at[idx],ph_recv.at[idx],(flip(di,masks,bits,1<<pp,ph),z))
        else:
            def zadd(stream, extra):
                zi=stream*ns+zz
                def fz():
                    waiting([],rz.at[zi],z_recv.at[zi])
                    @pl.loop(0,win//step)
                    def _(i):
                        r=pl.ds(i*step,step)
                        if s==0:
                            out[r]=out[r]+rz[zi,r].astype(jnp.float32)
                        else:
                            acc[slot,r]=(acc[slot,r].astype(jnp.float32)+rz[zi,r].astype(jnp.float32)).astype(acc.dtype)
                guard(conds+extra,fz)
            if sign>=0: zadd(0,[z>0])
            if sign<=0: zadd(1,[z<ns-1])
            if sign>0: send(conds,slot,rz.at[zz],z_recv.at[zz],(di,z+1))
            if sign<0: send(conds,slot,rz.at[ns+zz],z_recv.at[ns+zz],(di,z-1))
    for e in order:
        conds,cp=core(*e)
        guard(conds,lambda: cp.wait_send())
    for conds,cp in sends:
        guard(conds,lambda: cp.wait_send())

def scatter(plan, g):
    win,ns,ph,nslot=plan.win,plan.nseq,plan.phases,plan.slots
    nsend=len(plan.order())
    return pl.pallas_call(
        functools.partial(scatter_kernel,plan),
        out_shape=jax.ShapeDtypeStruct((win,8,LANES),jnp.float32),
        in_specs=[pl.BlockSpec(memory_space=pl.ANY)],
        out_specs=pl.BlockSpec(memory_space=pltpu.VMEM),
        scratch_shapes=[pltpu.VMEM((nslot,win,8,LANES),g.dtype),pltpu.VMEM((nslot,win,8,LANES),g.dtype),
            pltpu.VMEM(((2**ph-1)*ns,win,8,LANES),g.dtype),pltpu.VMEM((2*ns,win,8,LANES),g.dtype),
            pltpu.SemaphoreType.DMA((nslot,)),pltpu.SemaphoreType.DMA((nsend,)),
            pltpu.SemaphoreType.DMA((nslot,)),pltpu.SemaphoreType.DMA((nslot,)),
            pltpu.SemaphoreType.DMA(((2**ph-1)*ns,)),pltpu.SemaphoreType.DMA((2*ns,))],
        compiler_params=pltpu.CompilerParams(collective_id=1,has_side_effects=True,vmem_limit_bytes=48*1024*1024),
        name="scatter_grads",
    )(g)


def weight_kernel(plan, names, *refs):
    inputs = dict(zip(names, refs))
    out, mix = refs[len(names) :]
    rows = (((0,), (0,)), ((), ()))
    for name, shape in segments():
        first = plan.places[name]
        if math.prod(shape) < D * D:
            values = inputs[name + "0"]
            for r in range(-(-math.prod(shape) // LANES)):
                if name == "w_depth":
                    line = inputs[name + str(r)][...]
                else:
                    line = values[:, r * LANES : (r + 1) * LANES]
                tile, row = divmod(first + r, 8)
                out[tile, row : row + 1, : line.shape[1]] = line.astype(out.dtype)
            continue
        left, right = inputs[name + "0"], inputs[name + "1"]
        fold = shape[1] // LANES
        step = 256 if fold == 1 else 128

        @pl.loop(0, shape[0] // step)
        def _(i):
            part = left[:, pl.ds(pl.multiple_of(i * step, step), step)]
            value = lax.dot_general(part, right[...], rows, preferred_element_type=jnp.float32)
            if fold > 1:
                for j in range(fold):
                    for lane in range(LANES // 128):
                        at = j * LANES + lane * 128
                        mix[lane, pl.ds(j, step, stride=fold), :] = value[:, at : at + 128]
                value = jnp.concatenate([mix[lane, : step * fold] for lane in range(LANES // 128)], 1)
            tiles = step * fold // 8
            out[pl.ds(first // 8 + i * tiles, tiles)] = value.astype(out.dtype).reshape(tiles, 8, LANES)


def weight_grads(plan, gradients):
    names, operands = [], []
    for name, shape in segments():
        extent = math.prod(shape)
        if extent >= D * D:
            parts = gradients[name]
        elif name == "w_depth":
            parts = [value.reshape(1, D) for value in gradients[name]]
        else:
            parts = [gradients[name].reshape(1, extent)]
        for number, value in enumerate(parts):
            names.append(name + str(number))
            operands.append(value)
    vmem = pl.BlockSpec(memory_space=pltpu.VMEM)
    return pl.pallas_call(
        functools.partial(weight_kernel, plan, names),
        out_shape=jax.ShapeDtypeStruct((plan.padded, 8, LANES), jnp.bfloat16),
        in_specs=[vmem] * len(operands),
        out_specs=vmem,
        scratch_shapes=[pltpu.VMEM((LANES // 128, 512, 128), jnp.float32)],
        compiler_params=pltpu.CompilerParams(vmem_limit_bytes=60 * 1024 * 1024),
        name="weight_grads",
    )(*operands)


def sum_kernel(ndp, nseq, left, right, valid, out, part, line, cross, seq_send, seq_recv, dp_send, dp_recv):
    di, z = lax.axis_index(DP), lax.axis_index(SEQ)
    barrier = pltpu.get_barrier_semaphore()
    peers = [(di, lax.rem(z + i, nseq)) for i in range(1, nseq)]
    peers = peers + [(lax.rem(di + i, ndp), z) for i in range(1, ndp)]
    for peer in peers:
        pl.semaphore_signal(barrier, inc=1, device_id=peer, device_id_type=MESH)
    value, mask = left[...], valid[...]
    value = value * mask
    rows = [
        jnp.sum(value, 0, keepdims=True),
        jnp.sum(value * right[...], 0, keepdims=True),
        jnp.broadcast_to(jnp.sum(mask, 0, keepdims=True), (1, LANES)),
        jnp.zeros((5, LANES), jnp.float32),
    ]
    part[...] = jnp.concatenate(rows, 0)
    pl.semaphore_wait(barrier, len(peers))

    def exchange(count, me, target, slots, send, recv):
        copies = []
        for i in range(1, count):
            copy = pltpu.make_async_remote_copy(
                src_ref=part, dst_ref=slots.at[me], send_sem=send.at[i], recv_sem=recv.at[me],
                device_id=target(lax.rem(me + i, count)), device_id_type=MESH,
            )
            copy.start()
            copies.append(copy)
        slots[me] = part[...]
        for i in range(1, count):
            source = lax.rem(me + count - i, count)
            pltpu.make_async_remote_copy(
                src_ref=part, dst_ref=slots.at[source], send_sem=send.at[i], recv_sem=recv.at[source],
                device_id=(di, z), device_id_type=MESH,
            ).wait_recv()
        for copy in copies:
            copy.wait_send()
        total = slots[0]
        for i in range(1, count):
            total = total + slots[i]
        return total

    part[...] = exchange(nseq, z, lambda i: (di, i), line, seq_send, seq_recv)
    out[...] = exchange(ndp, di, lambda i: (i, z), cross, dp_send, dp_recv)


def batch_sums(left, right, valid, number):
    ndp, nseq = lax.axis_size(DP), lax.axis_size(SEQ)
    vmem = pl.BlockSpec(memory_space=pltpu.VMEM)
    return pl.pallas_call(
        functools.partial(sum_kernel, ndp, nseq),
        out_shape=jax.ShapeDtypeStruct((8, LANES), jnp.float32),
        in_specs=[vmem] * 3,
        out_specs=vmem,
        scratch_shapes=[
            pltpu.VMEM((8, LANES), jnp.float32),
            pltpu.VMEM((nseq, 8, LANES), jnp.float32),
            pltpu.VMEM((ndp, 8, LANES), jnp.float32),
            pltpu.SemaphoreType.DMA((nseq,)),
            pltpu.SemaphoreType.DMA((nseq,)),
            pltpu.SemaphoreType.DMA((ndp,)),
            pltpu.SemaphoreType.DMA((ndp,)),
        ],
        compiler_params=pltpu.CompilerParams(collective_id=number, has_side_effects=True),
        name="batch_sums" + str(number),
    )(left, right, valid)


def bucket_window(rel_bucket, block_len, full_len):
    first_pos = lax.axis_index(SEQ) * block_len
    width = -(-(block_len + full_len - 1) // 128) * 128
    padded = jnp.concatenate([rel_bucket, jnp.full((width,), -1, jnp.int32)])
    window = lax.dynamic_slice(padded, (full_len - block_len - first_pos,), (width,))
    return (window[:, None] == jnp.arange(NB, dtype=jnp.int32)[None, :]).astype(jnp.float32)


def head_scores(q, k, table, valid, head):
    block, width = q.shape[0], table.shape[1]
    full = k.shape[0]
    scores = lax.dot_general(q, k, (((1,), (1,)), ((), ())), preferred_element_type=jnp.float32)
    spread = jnp.broadcast_to(table[head : head + 1], (block, width))
    bias = pltpu.roll(spread, width - block + 1, 1, stride=1, stride_axis=0)[:, :full]
    return jnp.where(valid, scores * (1.0 / math.sqrt(HD)) + bias, -jnp.inf)


def attend_kernel(len_ref, q_ref, k_ref, v_ref, t_ref, ctx_ref, lse_ref):
    full = k_ref.shape[1]
    block = q_ref.shape[1]
    valid = lax.broadcasted_iota(jnp.int32, (1, full), 1) < len_ref[pl.program_id(0)]
    lane = lax.broadcasted_iota(jnp.int32, (block, 128), 1)
    lse = jnp.zeros((block, 128), jnp.float32)
    for h in range(H):
        cols = slice(h * HD, (h + 1) * HD)
        scores = head_scores(q_ref[0, :, cols], k_ref[0, :, cols], t_ref[...], valid, h)
        top = jnp.max(scores, -1, keepdims=True)
        weights = jnp.exp(scores - top)
        total = jnp.sum(weights, -1, keepdims=True)
        probs = (weights * (1.0 / total)).astype(jnp.bfloat16)
        ctx = jnp.dot(probs, v_ref[0, :, cols], preferred_element_type=jnp.float32)
        ctx_ref[0, :, cols] = ctx.astype(jnp.bfloat16)
        lse = jnp.where(lane == h, top + jnp.log(total), lse)
    lse_ref[0] = lse


def attend_back_kernel(len_ref, q_ref, k_ref, v_ref, t_ref, lse_ref, dctx_ref,
                       dq_ref, dk_ref, dv_ref, dt_ref, sums_ref):
    full = k_ref.shape[1]
    block = q_ref.shape[1]
    width = t_ref.shape[1]
    seq_id = pl.program_id(0)

    @pl.when(seq_id == 0)
    def _():
        dt_ref[...] = jnp.zeros_like(dt_ref)
        sums_ref[...] = jnp.zeros_like(sums_ref)

    valid = lax.broadcasted_iota(jnp.int32, (1, full), 1) < len_ref[seq_id]
    rows = (((0,), (0,)), ((), ()))
    for h in range(H):
        cols = slice(h * HD, (h + 1) * HD)
        q, k, v = q_ref[0, :, cols], k_ref[0, :, cols], v_ref[0, :, cols]
        dctx = dctx_ref[0, :, cols]
        scores = head_scores(q, k, t_ref[...], valid, h)
        probs = jnp.exp(scores - lse_ref[0, :, h : h + 1])
        d_probs = lax.dot_general(dctx, v, (((1,), (1,)), ((), ())), preferred_element_type=jnp.float32)
        delta = jnp.sum(probs * d_probs, -1, keepdims=True)
        d_scores = probs * (d_probs - delta)
        d_scores_b = d_scores.astype(jnp.bfloat16)
        dq = jnp.dot(d_scores_b, k, preferred_element_type=jnp.float32) * (1.0 / math.sqrt(HD))
        dk = lax.dot_general(d_scores_b, q, rows, preferred_element_type=jnp.float32)
        dv = lax.dot_general(probs.astype(jnp.bfloat16), dctx, rows, preferred_element_type=jnp.float32)
        dq_ref[0, :, cols] = dq.astype(jnp.bfloat16)
        dk_ref[0, :, cols] = (dk * (1.0 / math.sqrt(HD))).astype(jnp.bfloat16)
        dv_ref[0, :, cols] = dv.astype(jnp.bfloat16)
        sums_ref[0:1, cols] += jnp.sum(dq, 0, keepdims=True)
        sums_ref[1:2, cols] += jnp.sum(dv, 0, keepdims=True)
        wide = jnp.concatenate([d_scores, jnp.zeros((block, width - full), jnp.float32)], 1)
        folded = wide[0:8]
        folded = pltpu.roll(folded, block - 1, 1)
        for g in range(1, block // 8):
            folded = folded + pltpu.roll(wide[8 * g : 8 * g + 8], block - 1 - 8 * g, 1)
        line = folded[0:1]
        for r in range(1, 8):
            line = line + pltpu.roll(folded[r : r + 1], width - r, 1)
        dt_ref[h : h + 1, :] += line


def attend(lengths, queries, keys, values, table):
    seqs, block, width = queries.shape
    full = keys.shape[1]
    return pl.pallas_call(
        attend_kernel,
        grid_spec=pltpu.PrefetchScalarGridSpec(
            num_scalar_prefetch=1,
            grid=(seqs,),
            in_specs=[
                pl.BlockSpec((1, block, width), lambda s, n: (s, 0, 0)),
                pl.BlockSpec((1, full, width), lambda s, n: (s, 0, 0)),
                pl.BlockSpec((1, full, width), lambda s, n: (s, 0, 0)),
                pl.BlockSpec(table.shape, lambda s, n: (0, 0)),
            ],
            out_specs=[
                pl.BlockSpec((1, block, width), lambda s, n: (s, 0, 0)),
                pl.BlockSpec((1, block, 128), lambda s, n: (s, 0, 0)),
            ],
        ),
        out_shape=[
            jax.ShapeDtypeStruct((seqs, block, width), jnp.bfloat16),
            jax.ShapeDtypeStruct((seqs, block, 128), jnp.float32),
        ],
        name="attend",
    )(lengths, queries, keys, values, table)


def attend_back(lengths, queries, keys, values, table, lse, d_context):
    seqs, block, width = queries.shape
    full = keys.shape[1]
    return pl.pallas_call(
        attend_back_kernel,
        grid_spec=pltpu.PrefetchScalarGridSpec(
            num_scalar_prefetch=1,
            grid=(seqs,),
            in_specs=[
                pl.BlockSpec((1, block, width), lambda s, n: (s, 0, 0)),
                pl.BlockSpec((1, full, width), lambda s, n: (s, 0, 0)),
                pl.BlockSpec((1, full, width), lambda s, n: (s, 0, 0)),
                pl.BlockSpec(table.shape, lambda s, n: (0, 0)),
                pl.BlockSpec((1, block, 128), lambda s, n: (s, 0, 0)),
                pl.BlockSpec((1, block, width), lambda s, n: (s, 0, 0)),
            ],
            out_specs=[
                pl.BlockSpec((1, block, width), lambda s, n: (s, 0, 0)),
                pl.BlockSpec((1, full, width), lambda s, n: (s, 0, 0)),
                pl.BlockSpec((1, full, width), lambda s, n: (s, 0, 0)),
                pl.BlockSpec(table.shape, lambda s, n: (0, 0)),
                pl.BlockSpec((8, width), lambda s, n: (0, 0)),
            ],
        ),
        out_shape=[
            jax.ShapeDtypeStruct((seqs, block, width), jnp.bfloat16),
            jax.ShapeDtypeStruct((seqs, full, width), jnp.bfloat16),
            jax.ShapeDtypeStruct((seqs, full, width), jnp.bfloat16),
            jax.ShapeDtypeStruct(table.shape, jnp.float32),
            jax.ShapeDtypeStruct((8, width), jnp.float32),
        ],
        name="attend_back",
    )(lengths, queries, keys, values, table, lse, d_context)


def seq_gather(rows, seq_count):
    return lax.all_gather(rows.reshape(seq_count, -1, D), SEQ, axis=1, tiled=True)


def seq_scatter(rows):
    return lax.psum_scatter(rows, SEQ, scatter_dimension=1, tiled=True)


def attend_forward(stream, weights, lengths, onehot, seq_count):
    normed_b = norm_rows(
        stream, vector(weights, "attn_ng"), vector(weights, "attn_nb")
    ).astype(jnp.bfloat16)
    normed_all = seq_gather(normed_b, seq_count)
    queries = (forward_dot(normed_b, weights["w_q"]) + vector(weights, "b_q")).astype(
        jnp.bfloat16
    )
    flat_all = normed_all.reshape(-1, D)
    keys = forward_dot(flat_all, weights["w_k"]).astype(jnp.bfloat16)
    values = (forward_dot(flat_all, weights["w_v"]) + vector(weights, "b_v")).astype(
        jnp.bfloat16
    )
    table = lax.dot_general(
        weights["rel"], onehot.astype(jnp.bfloat16), (((0,), (1,)), ((), ())),
        preferred_element_type=jnp.float32,
    )
    queries3 = queries.reshape(seq_count, -1, D)
    keys3 = keys.reshape(seq_count, -1, D)
    values3 = values.reshape(seq_count, -1, D)
    context, lse = attend(lengths, queries3, keys3, values3, table)
    context = context.reshape(-1, D)
    output = stream + forward_dot(context, weights["w_o"]) + vector(weights, "b_o")
    return (output, (normed_b, flat_all, queries3, keys3, values3, table, lse, context))


def attend_backward(stream, weights, stored, grad_out, lengths, onehot):
    normed_b, flat_all, queries3, keys3, values3, table, lse, context = stored
    grad_b = grad_out.astype(jnp.bfloat16)
    gradients = {"w_o": (context, grad_b), "b_o": jnp.sum(grad_out, 0)}
    d_context = back_dot(grad_b, weights["w_o"]).astype(jnp.bfloat16).reshape(queries3.shape)
    dq, dk, dv, dt, sums = attend_back(lengths, queries3, keys3, values3, table, lse, d_context)
    gradients["rel"] = lax.dot_general(
        onehot, dt, (((0,), (1,)), ((), ())), precision=lax.Precision.HIGHEST
    )
    query_b, key_b, value_b = dq.reshape(-1, D), dk.reshape(-1, D), dv.reshape(-1, D)
    remote = back_dot(key_b, weights["w_k"]) + back_dot(value_b, weights["w_v"])
    remote = seq_scatter(remote.astype(jnp.bfloat16).reshape(keys3.shape)).reshape(stream.shape)
    gradients["w_q"] = (normed_b, query_b)
    gradients["b_q"] = sums[0]
    gradients["w_k"] = (flat_all, key_b)
    gradients["w_v"] = (flat_all, value_b)
    gradients["b_v"] = sums[1]
    d_normed = back_dot(query_b, weights["w_q"]) + remote.astype(jnp.float32)
    d_stream, gain_grad, shift_grad = norm_back(
        stream, vector(weights, "attn_ng"), vector(weights, "attn_nb"), d_normed
    )
    gradients["attn_ng"] = gain_grad
    gradients["attn_nb"] = shift_grad
    return (grad_out + d_stream, gradients)


def depthwise(padded, kernel):
    length = padded.shape[1] - kernel.shape[0] + 1
    summed = jnp.zeros((padded.shape[0], length, padded.shape[2]), jnp.float32)
    for offset in range(kernel.shape[0]):
        summed = summed + kernel[offset] * padded[:, offset : offset + length]
    return summed.reshape(-1, padded.shape[2])


def depth_back(padded, d_depth3, d_padded, kernel):
    length = d_depth3.shape[1]
    taps_count = kernel.shape[0]
    kernel_grad = [
        jnp.sum(padded[:, offset : offset + length] * d_depth3, (0, 1))
        for offset in range(taps_count)
    ]
    d_gated = jnp.zeros(d_depth3.shape, jnp.float32)
    for offset in range(taps_count):
        start_at = taps_count - 1 - offset
        d_gated = d_gated + kernel[offset] * d_padded[:, start_at : start_at + length]
    return (kernel_grad, d_gated.reshape(-1, d_depth3.shape[2]))


def conv_front(stream, weights, valid_rows, seq_count):
    normed_b = norm_rows(
        stream, vector(weights, "conv_ng"), vector(weights, "conv_nb")
    ).astype(jnp.bfloat16)
    pre_gate = forward_dot(normed_b, weights["w_pi"]) + vector(weights, "b_pi")
    gated = pre_gate[:, :D] * jax.nn.sigmoid(pre_gate[:, D:]) * valid_rows[:, None]
    padded = with_halo(gated.reshape(seq_count, -1, D), ((SEQ, 1),), K // 2)
    depth = depthwise(padded, vector(weights, "w_depth"))
    return (normed_b, pre_gate, padded, depth)


def conv_tail(stream, weights, depth, batch_mean, inv_std):
    standard = (depth - batch_mean) * inv_std
    normed_bn = standard * vector(weights, "bng") + vector(weights, "bnb")
    active = swish_act(normed_bn).astype(jnp.bfloat16)
    output = stream + forward_dot(active, weights["w_po"]) + vector(weights, "b_po")
    return (output, (standard, normed_bn, active))


def conv_tail_back(weights, stored, grad_out, valid_rows):
    standard, normed_bn, active = stored
    grad_b = grad_out.astype(jnp.bfloat16)
    gradients = {"w_po": (active, grad_b), "b_po": jnp.sum(grad_out, 0)}
    d_normed = back_dot(grad_b, weights["w_po"]) * swish_grad(normed_bn)
    gradients["bng"] = jnp.sum(d_normed * standard, 0)
    gradients["bnb"] = jnp.sum(d_normed, 0)
    d_standard = d_normed * vector(weights, "bng") * valid_rows[:, None]
    return (d_standard, gradients)


def gate_back(stream, weights, normed_b, pre_gate, d_gated, valid_rows, grad_out, kernel_grad):
    linear_half = pre_gate[:, :D]
    gate_sig = jax.nn.sigmoid(pre_gate[:, D:])
    d_gated = d_gated * valid_rows[:, None]
    d_pre = jnp.concatenate(
        [d_gated * gate_sig, d_gated * linear_half * gate_sig * (1.0 - gate_sig)], 1
    )
    d_pre_b = d_pre.astype(jnp.bfloat16)
    gradients = {
        "w_depth": kernel_grad,
        "w_pi": (normed_b, d_pre_b),
        "b_pi": jnp.sum(d_pre, 0),
    }
    d_normed = back_dot(d_pre_b, weights["w_pi"])
    d_stream, gain_grad, shift_grad = norm_back(
        stream, vector(weights, "conv_ng"), vector(weights, "conv_nb"), d_normed
    )
    gradients["conv_ng"] = gain_grad
    gradients["conv_nb"] = shift_grad
    return (grad_out + d_stream, gradients)


def conv_front_back(stream, weights, stored, d_depth, valid_rows, grad_out, seq_count):
    normed_b, pre_gate, padded, depth = stored
    d_depth3 = d_depth.reshape(seq_count, -1, D)
    d_padded = with_halo(d_depth3, ((SEQ, 1),), K // 2)
    kernel_grad, d_gated = depth_back(padded, d_depth3, d_padded, vector(weights, "w_depth"))
    return gate_back(
        stream, weights, normed_b, pre_gate, d_gated, valid_rows, grad_out, kernel_grad
    )


def adam_update(param_vec, grad_in, first_mom, second):
    new_first = BETA_ONE * first_mom + (1.0 - BETA_ONE) * grad_in
    new_second = BETA_TWO * second + (1.0 - BETA_TWO) * grad_in * grad_in
    corr_one = 1.0 - BETA_ONE**STEP
    corr_two = 1.0 - BETA_TWO**STEP
    step_size = new_first / corr_one / (jnp.sqrt(new_second / corr_two) + ADAM_EPS)
    return (param_vec - LEARN_RATE * (step_size + DECAY * param_vec), new_first, new_second)


def per_device(inputs, lengths, rel_bucket, params, moment_one, moment_two, cotangent):
    seq_count, block_len, model_width = inputs.shape
    full_len = block_len * lax.axis_size(SEQ)
    first_pos = lax.axis_index(SEQ) * block_len
    positions = first_pos + jnp.arange(block_len, dtype=jnp.int32)
    valid_own = positions[None, :] < lengths[:, None]
    valid_rows = valid_own.astype(jnp.float32).reshape(-1)
    onehot = bucket_window(rel_bucket, block_len, full_len)
    plan = Plan(lax.axis_size(DP), lax.axis_size(SEQ), params.shape[0])
    gathered = gather(plan, own_block(plan, params))
    weights = unpack(gathered.reshape(-1, LANES))
    stream0 = inputs.reshape(-1, model_width)
    stream1, stored1 = ffn_forward(stream0, weights, "first")
    stream2, stored2 = attend_forward(stream1, weights, lengths, onehot, seq_count)
    stored3 = conv_front(stream2, weights, valid_rows, seq_count)
    depth = stored3[3]
    valid_column = valid_rows[:, None]
    sums = batch_sums(depth, depth, valid_column, 2)
    first_sum, square_sum, token_count = sums[0], sums[1], sums[2, 0]
    batch_mean = first_sum / token_count
    inv_std = lax.rsqrt(square_sum / token_count - batch_mean * batch_mean + BATCH_EPS)
    stream3, stored4 = conv_tail(stream2, weights, depth, batch_mean, inv_std)
    stream4, stored5 = ffn_forward(stream3, weights, "second")
    output = norm_rows(stream4, vector(weights, "fin_g"), vector(weights, "fin_b"))
    grad_out = cotangent.reshape(-1, model_width) * valid_rows[:, None]
    d_stream4, gain_grad, shift_grad = norm_back(
        stream4, vector(weights, "fin_g"), vector(weights, "fin_b"), grad_out
    )
    gradients = {"fin_g": gain_grad, "fin_b": shift_grad}
    d_stream3, partial_grads = ffn_backward(stream3, weights, "second", stored5, d_stream4)
    gradients.update(partial_grads)
    d_standard, partial_grads = conv_tail_back(weights, stored4, d_stream3, valid_rows)
    gradients.update(partial_grads)
    standard = stored4[0]
    sums = batch_sums(d_standard, standard, valid_column, 3)
    sum_dz, sum_dzz = sums[0], sums[1]
    d_depth = (
        valid_rows[:, None]
        * inv_std
        * (d_standard - sum_dz / token_count - standard * sum_dzz / token_count)
    )
    d_stream2, partial_grads = conv_front_back(
        stream2, weights, stored3, d_depth, valid_rows, d_stream3, seq_count
    )
    gradients.update(partial_grads)
    d_stream1, partial_grads = attend_backward(
        stream1, weights, stored2, d_stream2, lengths, onehot
    )
    gradients.update(partial_grads)
    d_stream0, partial_grads = ffn_backward(stream0, weights, "first", stored1, d_stream1)
    gradients.update(partial_grads)
    window = scatter(plan, weight_grads(plan, gradients))
    grad_shard = own_shard(plan, window)
    new_params, new_first, new_second = adam_update(params, grad_shard, moment_one, moment_two)
    return (
        output.reshape(inputs.shape),
        d_stream0.reshape(inputs.shape),
        grad_shard,
        new_params,
        new_first,
        new_second,
    )


def solution(mesh):
    return jax.shard_map(
        per_device,
        mesh=mesh,
        in_specs=(
            P(DP, SEQ, None),
            P(DP),
            P(),
            P((DP, SEQ)),
            P((DP, SEQ)),
            P((DP, SEQ)),
            P(DP, SEQ, None),
        ),
        out_specs=(
            P(DP, SEQ, None),
            P(DP, SEQ, None),
            P((DP, SEQ)),
            P((DP, SEQ)),
            P((DP, SEQ)),
            P((DP, SEQ)),
        ),
        check_vma=False,
    )
```

profile of v0, /device:TPU:9, one launch (start us, length us, event | category | flops | bytes accessed | tf_op | source)
XLA Modules:
  0.0 448.7 jit_solution(17810746655320583031)
XLA Ops:
  17.0 6.2 %concatenate.79 = bf16[200192]{0:T(1024)(128)(2,1)S(1)} concatenate(bf16[3584]{0:T(1024)(128)(2,1)S(1)} %broadcast_in_dim.24, f32[189368]{0:T(1024)} %param.12, bf16[4096]{0:T(1024)(128)(2,1)S(1)} %collective-permute-done, bf16[3144]{0:T(1024)(128)(2,1)S(1)} %broadcast_in_dim.25), dimensions={0} | concatenate | bytes 1179504 | tf_op jit(solution)/shard_map/concatenate | solution.py:124
  25.4 62.2 %gather_params.1 = bf16[1486,8,512]{2,1,0:T(8,128)(2,1)} custom-call(bf16[47,8,512]{2,1,0:T(8,128)(2,1)} %reshape.607.src), custom_call_target="tpu_custom_call" | custom-call | tf_op jit(solution)/shard_map/gather_params/pallas_call | solution.py:383
  90.6 4.6 %fusion.198 = (bf16[256,8,512]{2,1,0:T(8,128)(2,1)}, bf16[256,8,512]{2,1,0:T(8,128)(2,1)}) fusion(bf16[1486,8,512]{2,1,0:T(8,128)(2,1)} %gather_params.1), kind=kLoop, calls=%fused_computation.429 | loop fusion | bytes 8388608 | tf_op jit(solution)/shard_map/slice | solution.py:106
  95.1 4.4 reshape.609
  99.8 4.5 %multiply_convert_fusion.1 = (bf16[384,2048]{1,0:T(8,128)(2,1)S(1)}, f32[384,2048]{1,0:T(8,128)}) fusion(f32[2048]{0:T(1024)S(1)} %bitcast.450, bf16[384,512]{1,0:T(8,128)(2,1)S(1)} %bitcast.310, bf16[512,2048]{1,0:T(8,128)(2,1)} %reshape.609), kind=kOutput, calls=%fused_computation.62 | convolution fusion | flops 810024960 | bytes 7217152 | tf_op jit(solution)/shard_map/dot_general | solution.py:167
  104.3 3.3 fusion.208
  119.4 28.8 %all-gather.2.cloned.1.call-done = bf16[2,768,512]{2,1,0:T(8,128)(2,1)} async-done(((bf16[2,192,512]{2,1,0:T(8,128)(2,1)}), bf16[2,768,512]{2,1,0:T(8,128)(2,1)}) %all-gather.2.cloned.1.call-update) | async-done | bytes 1572880 | tf_op jit(solution)/shard_map/all_gather | solution.py:782
  148.2 3.8 convolution_convert_fusion
  155.3 13.0 %attend.1 = (bf16[2,192,512]{2,1,0:T(8,128)(2,1)}, f32[2,192,128]{2,1,0:T(8,128)}) custom-call(s32[2]{0:T(128)} %len_ref.3, bf16[2,192,512]{2,1,0:T(8,128)(2,1)} %bitcast.303, bf16[2,768,512]{2,1,0:T(8,128)(2,1)} %bitcast.294, bf16[2,768,512]{2,1,0:T(8,128)(2,1)} %bitcast.296, f32[8,1024]{1,0:T(8,128)} %fusion.181.t_ref), custom_call_target="tpu_custom_call" | custom-call | tf_op jit(solution)/shard_map/attend/pallas_call | solution.py:722
  180.7 4.7 %reshape.620 = bf16[512,2048]{1,0:T(8,128)(2,1)} reshape(bf16[256,8,512]{2,1,0:T(8,128)(2,1)} %get-tuple-element.112) | data formatting | bytes 4194304 | tf_op jit(solution)/shard_map/reshape | solution.py:109
  185.5 6.7 %multiply_add_fusion.2 = f32[2,192,512]{2,1,0:T(8,128)} fusion(f32[2,192,512]{2,1,0:T(8,128)S(1)} %bitcast.271, f32[2,15,512]{2,1,0:T(8,128)} %collective-permute-done.1, f32[2,15,512]{2,1,0:T(8,128)} %collective-permute-done.2, f32[512]{0:T(512)} %bitcast.338, f32[512]{0:T(512)} %bitcast.340, f32[512]{0:T(512)} %bitcast.342, f32[512]{0:T(512)} %bitcast.344, ...), kind=kLoop, calls=%fused_computation.315 | loop fusion | flops 17891328 | bytes 1759232 | tf_op jit(solution)/shard_map/add | solution.py:845
  192.2 12.7 %batch_sums2.1 = f32[8,512]{1,0:T(8,128)} custom-call(f32[384,512]{1,0:T(8,128)} %bitcast.282, f32[384,512]{1,0:T(8,128)} %bitcast.283, f32[384,1]{1,0:T(8,128)} %reshape.707.valid), custom_call_target="tpu_custom_call" | custom-call | tf_op jit(solution)/shard_map/batch_sums2/pallas_call | solution.py:621
  214.9 3.3 fusion.211
  221.4 3.9 fusion.199
  231.5 11.1 %batch_sums3.1 = f32[8,512]{1,0:T(8,128)} custom-call(f32[384,512]{1,0:T(8,128)} %get-tuple-element.187.left, f32[384,512]{1,0:T(8,128)} %copy-done.15, f32[384,1]{1,0:T(8,128)} %reshape.707.valid), custom_call_target="tpu_custom_call" | custom-call | tf_op jit(solution)/shard_map/batch_sums3/pallas_call | solution.py:621
  244.3 3.3 fusion.189
  256.0 3.6 fusion.38
  266.7 23.6 %attend_back.1 = (bf16[2,192,512]{2,1,0:T(8,128)(2,1)}, bf16[2,768,512]{2,1,0:T(8,128)(2,1)}, bf16[2,768,512]{2,1,0:T(8,128)(2,1)}, f32[8,1024]{1,0:T(8,128)}, f32[8,512]{1,0:T(8,128)}) custom-call(s32[2]{0:T(128)} %len_ref.3, bf16[2,192,512]{2,1,0:T(8,128)(2,1)} %bitcast.304, bf16[2,768,512]{2,1,0:T(8,128)(2,1)} %bitcast.295, ...), custom_call_target="tpu_custom_call" | custom-call | tf_op jit(solution)/shard_map/attend_back/pallas_call | solution.py:749
  293.0 3.4 fusion.1
  317.3 13.5 %reduce-scatter.2.cloned.1.call-done = bf16[2,192,512]{2,1,0:T(8,128)(2,1)} async-done(((bf16[2,768,512]{2,1,0:T(8,128)(2,1)}), bf16[2,192,512]{2,1,0:T(8,128)(2,1)}) %reduce-scatter.2.cloned.1.call-update) | async-done | bytes 393232 | tf_op jit(solution)/shard_map/reduce_scatter | solution.py:786
  335.1 4.0 fusion.200
  342.0 26.8 %weight_grads.1.g = bf16[1487,8,512]{2,1,0:T(8,128)(2,1)} custom-call(f32[1,512]{1,0:T(1,128)} %bitcast.459, f32[1,512]{1,0:T(1,128)} %bitcast.460, bf16[384,512]{1,0:T(8,128)(2,1)} %get-tuple-element.120.refs_2_, bf16[384,2048]{1,0:T(8,128)(2,1)} %copy-done.34, f32[1,2048]{1,0:T(1,128)} %bitcast.401, bf16[384,2048]{1,0:T(8,128)(2,1)} %copy-done.31, ...), custom_call_target="tpu_custom_call" | custom-call | tf_op jit(solution)/shard_map/weight_grads/pallas_call | solution.py:562
  368.8 67.5 %scatter_grads.1 = f32[48,8,512]{2,1,0:T(8,128)S(1)} custom-call(bf16[1487,8,512]{2,1,0:T(8,128)(2,1)} %weight_grads.1.g), custom_call_target="tpu_custom_call" | custom-call | tf_op jit(solution)/shard_map/scatter_grads/pallas_call | solution.py:499
  438.2 3.2 multiply_subtract_fusion
  (349 shorter events, 105.4 us)
Async XLA Ops:
  7.2 141.0 %all-gather.2.cloned.1.call-start = ((), (), s32[]{:S(2)}) async-start(), calls=%async_computation.1 | async-start | bytes 1966080 | tf_op jit(solution)/shard_map/all_gather | solution.py:782
  7.9 9.1 %collective-permute-start = (bf16[4096]{0:T(1024)(128)(2,1)S(1)}, bf16[4096]{0:T(1024)(128)(2,1)S(1)}, u32[]{:S(2)}, u32[]{:S(2)}) collective-permute-start(bf16[4096]{0:T(1024)(128)(2,1)S(1)} %slice.590), channel_id=1, source_target_pairs={{1,0},{2,1},{3,2},{4,3},{5,4},{6,5},{7,6},{8,7},{9,8},{10,9},{11,1... | collective-permute-start | bytes 24584 | tf_op jit(solution)/shard_map/ppermute | solution.py:120
  89.3 81.6 %copy-start.52 = (f32[1,512]{1,0:T(1,128)}, f32[1,512]{1,0:T(1,128)S(1)}, u32[]{:S(2)}) copy-start(f32[1,512]{1,0:T(1,128)S(1)} %get-tuple-element.101) | copy-start | bytes 6148
  107.6 60.7 %copy-start.4 = (f32[384,512]{1,0:T(8,128)}, f32[384,512]{1,0:T(8,128)S(1)}, u32[]{:S(2)}) copy-start(f32[384,512]{1,0:T(8,128)S(1)} %get-tuple-element.176) | copy-start | bytes 2359300
  108.9 221.9 %reduce-scatter.2.cloned.1.call-start = ((), (), s32[]{:S(2)}) async-start(), calls=%async_computation.2 | async-start | bytes 1966080 | tf_op jit(solution)/shard_map/reduce_scatter | solution.py:786
  110.3 41.7 %copy-start.109 = (s32[1024]{0:T(1024)}, s32[1024]{0:T(1024)S(1)}, u32[]{:S(2)}) copy-start(s32[1024]{0:T(1024)S(1)} %pad_dynamic-slice_fusion) | copy-start | bytes 12292
  116.6 35.5 %copy-start.38 = (f32[31,512]{1,0:T(8,128)}, f32[31,512]{1,0:T(8,128)S(1)}, u32[]{:S(2)}) copy-start(f32[31,512]{1,0:T(8,128)S(1)} %slice_convert_fusion) | copy-start | bytes 190468
  117.3 68.2 %copy-start.64 = (f32[1,512]{1,0:T(1,128)}, f32[1,512]{1,0:T(1,128)S(1)}, u32[]{:S(2)}) copy-start(f32[1,512]{1,0:T(1,128)S(1)} %get-tuple-element.130) | copy-start | bytes 6148
  170.0 41.3 %copy-start = (f32[384,512]{1,0:T(8,128)}, f32[384,512]{1,0:T(8,128)S(1)}, u32[]{:S(2)}) copy-start(f32[384,512]{1,0:T(8,128)S(1)} %get-tuple-element.178) | copy-start | bytes 2359300
  172.6 12.9 %collective-permute-start.1 = (f32[2,15,512]{2,1,0:T(8,128)}, f32[2,15,512]{2,1,0:T(8,128)}, u32[]{:S(2)}, u32[]{:S(2)}) collective-permute-start(f32[2,15,512]{2,1,0:T(8,128)} %get-tuple-element.129), channel_id=1, source_target_pairs={{0,1},{1,2},{2,3},{4,5},{5,6},{6,7},{8,9},{9,10},{10,11},{12,13},{... | collective-permute-start | bytes 184328 | tf_op jit(solution)/shard_map/ppermute | solution.py:38
  175.8 9.7 %collective-permute-start.2 = (f32[2,15,512]{2,1,0:T(8,128)}, f32[2,15,512]{2,1,0:T(8,128)}, u32[]{:S(2)}, u32[]{:S(2)}) collective-permute-start(f32[2,15,512]{2,1,0:T(8,128)} %get-tuple-element.128), channel_id=1, source_target_pairs={{1,0},{2,1},{3,2},{5,4},{6,5},{7,6},{9,8},{10,9},{11,10},{13,12},{... | collective-permute-start | bytes 184328 | tf_op jit(solution)/shard_map/ppermute | solution.py:39
  185.4 23.5 %copy-start.54 = (f32[1,512]{1,0:T(1,128)S(1)}, f32[1,512]{1,0:T(1,128)}, u32[]{:S(2)}) copy-start(f32[1,512]{1,0:T(1,128)} %get-tuple-element.98) | copy-start | bytes 6148
  185.4 23.5 %copy-start.56 = (f32[1,512]{1,0:T(1,128)S(1)}, f32[1,512]{1,0:T(1,128)}, u32[]{:S(2)}) copy-start(f32[1,512]{1,0:T(1,128)} %get-tuple-element.99) | copy-start | bytes 6148
  185.5 25.8 %copy-start.100 = (f32[1,512]{1,0:T(1,128)S(1)}, f32[1,512]{1,0:T(1,128)}, u32[]{:S(2)}) copy-start(f32[1,512]{1,0:T(1,128)} %get-tuple-element.97) | copy-start | bytes 6148
  247.6 5.5 %collective-permute-start.4 = (f32[2,15,512]{2,1,0:T(8,128)S(1)}, f32[2,15,512]{2,1,0:T(8,128)S(1)}, u32[]{:S(2)}, u32[]{:S(2)}) collective-permute-start(f32[2,15,512]{2,1,0:T(8,128)S(1)} %get-tuple-element.127), channel_id=1, source_target_pairs={{0,1},{1,2},{2,3},{4,5},{5,6},{6,7},{8,9},{9,10},{10,11},{12,13},{... | collective-permute-start | bytes 184328 | tf_op jit(solution)/shard_map/ppermute | solution.py:38
  250.7 5.0 %collective-permute-start.3 = (f32[2,15,512]{2,1,0:T(8,128)S(1)}, f32[2,15,512]{2,1,0:T(8,128)S(1)}, u32[]{:S(2)}, u32[]{:S(2)}) collective-permute-start(f32[2,15,512]{2,1,0:T(8,128)S(1)} %get-tuple-element.126), channel_id=1, source_target_pairs={{1,0},{2,1},{3,2},{5,4},{6,5},{7,6},{9,8},{10,9},{11,10},{13,12},{... | collective-permute-start | bytes 184328 | tf_op jit(solution)/shard_map/ppermute | solution.py:39
  264.0 26.2 %copy-start.11 = (f32[384,512]{1,0:T(8,128)}, f32[384,512]{1,0:T(8,128)S(1)}, u32[]{:S(2)}) copy-start(f32[384,512]{1,0:T(8,128)S(1)} %get-tuple-element.77) | copy-start | bytes 2359300
  264.1 28.9 %copy-start.29 = (bf16[384,512]{1,0:T(8,128)(2,1)}, bf16[384,512]{1,0:T(8,128)(2,1)S(1)}, u32[]{:S(2)}) copy-start(bf16[384,512]{1,0:T(8,128)(2,1)S(1)} %convert_element_type.208.refs_19_) | copy-start | bytes 1179652
  304.7 26.1 %copy-start.5 = (f32[384,512]{1,0:T(8,128)S(1)}, f32[384,512]{1,0:T(8,128)}, u32[]{:S(2)}) copy-start(f32[384,512]{1,0:T(8,128)} %copy-done.4) | copy-start | bytes 2359300
  304.7 26.1 %copy-start.37 = (bf16[2,192,512]{2,1,0:T(8,128)(2,1)S(1)}, bf16[2,192,512]{2,1,0:T(8,128)(2,1)}, u32[]{:S(2)}) copy-start(bf16[2,192,512]{2,1,0:T(8,128)(2,1)} %get-tuple-element.15) | copy-start | bytes 1179652
  304.7 26.1 %copy-start.41 = (f32[384]{0:T(512)S(1)}, f32[384]{0:T(512)}, u32[]{:S(2)}) copy-start(f32[384]{0:T(512)} %copy-done.40) | copy-start | bytes 4612
  304.7 26.1 %copy-start.51 = (f32[1,512]{1,0:T(1,128)S(1)}, f32[1,512]{1,0:T(1,128)}, u32[]{:S(2)}) copy-start(f32[1,512]{1,0:T(1,128)} %copy-done.50) | copy-start | bytes 6148
  309.9 23.3 %copy-start.45 = (f32[384]{0:T(512)S(1)}, f32[384]{0:T(512)}, u32[]{:S(2)}) copy-start(f32[384]{0:T(512)} %copy-done.44) | copy-start | bytes 4612
  312.9 20.4 %copy-start.61 = (f32[384]{0:T(512)S(1)}, f32[384]{0:T(512)}, u32[]{:S(2)}) copy-start(f32[384]{0:T(512)} %copy-done.60) | copy-start | bytes 4612
  (97 other events, 728.3 us)
Sparse Core Ops, SparseCore 0:
  109.0 39.1 all-gather.1
  296.6 34.2 reduce-scatter.1
where the time goes:
time: 458 us; the launch traced here: 449 us
  Pallas kernels  217 us (47%)
  other arithmetic  56.3 us (12%)
  matrix products  54.8 us (12%)
  waiting for transfers between devices  44.9 us (10%)
  local copies, waits for them, and re-layouts  41.1 us (9%)
  between operations  21.2 us (5%)
  starting transfers between devices  13.5 us (3%)
    pallas_call x1, Pallas kernels, scatter(): pl.pallas_call(functools.partial(scatter_kernel, plan), out_shape=jax.Sha...  67.5 us
    pallas_call x1, Pallas kernels, gather(): pl.pallas_call(functools.partial(gather_kernel, plan), out_shape=jax.Shap...  62.2 us
    all_gather x1, waiting for transfers between devices, seq_gather(): lax.all_gather(rows.reshape(seq_count, -1, D), SEQ, axis=1, tiled=True)  28.8 us
    dot_general x10, matrix products, back_dot(): lax.dot_general(grad_in, weight, (((1,), (1,)), ((), ())), preferred_elem...  27.6 us
    pallas_call x1, Pallas kernels, weight_grads(): pl.pallas_call(functools.partial(weight_kernel, plan, names), out_shape=j...  26.8 us
    dot_general x10, matrix products, forward_dot(): return jnp.dot(left_mat, weight, preferred_element_type=jnp.float32)  25.6 us
    pallas_call x2, Pallas kernels, batch_sums(): pl.pallas_call(functools.partial(sum_kernel, ndp, nseq), out_shape=jax.Sh...  23.8 us
    pallas_call x1, Pallas kernels, attend_back(): pl.pallas_call(attend_back_kernel, grid_spec=pltpu.PrefetchScalarGridSpec...  23.6 us
  transfers between devices with their start and end apart: 7, of which 3 were waited for; matrix products, arithmetic and copies ran while one was open for 9% of the time, Pallas kernels for 0%

commit v1 on v0

--- a/solution.py
+++ b/solution.py
@@ -26,19 +26,6 @@
 BETA_ONE = 0.9
 BETA_TWO = 0.98
 ADAM_EPS = 1e-08
-
-
-def with_halo(shard, sides, width):
-    for axis, dim in sides:
-        devices, length = (lax.axis_size(axis), shard.shape[dim])
-        up = [(i, (i + 1) % devices) for i in range(devices - 1)]
-        down = [(j, i) for i, j in up]
-        last = lax.slice_in_dim(shard, length - width, length, axis=dim)
-        leading = lax.slice_in_dim(shard, 0, width, axis=dim)
-        before = lax.ppermute(last, axis, up)
-        after = lax.ppermute(leading, axis, down)
-        shard = jnp.concatenate([before, shard, after], axis=dim)
-    return shard
 
 
 def segments():
@@ -152,67 +139,14 @@
     return sig_vals * (1.0 + values * (1.0 - sig_vals))
 
 
-def norm_rows(values, scale_vec, shift_vec):
-    centre = values - jnp.mean(values, -1, keepdims=True)
-    spread = jnp.mean(centre * centre, -1, keepdims=True)
-    return centre * lax.rsqrt(spread + NORM_EPS) * scale_vec + shift_vec
-
-
-def norm_back(values, scale_vec, shift_vec, grad_out):
-    _, pullback = jax.vjp(norm_rows, values, scale_vec, shift_vec)
-    return pullback(grad_out)
-
-
 def forward_dot(left_mat, weight):
     return jnp.dot(left_mat, weight, preferred_element_type=jnp.float32)
-
-
-def cross_dot(left_mat, right_mat):
-    return lax.dot_general(
-        left_mat, right_mat, (((0,), (0,)), ((), ())), preferred_element_type=jnp.float32
-    )
 
 
 def back_dot(grad_in, weight):
     return lax.dot_general(
         grad_in, weight, (((1,), (1,)), ((), ())), preferred_element_type=jnp.float32
     )
-
-
-def ffn_forward(stream, weights, prefix):
-    normed_b = norm_rows(
-        stream, vector(weights, prefix + "_ng"), vector(weights, prefix + "_nb")
-    ).astype(jnp.bfloat16)
-    hidden = forward_dot(normed_b, weights[prefix + "_w_in"]) + vector(weights, prefix + "_b_in")
-    active = swish_act(hidden).astype(jnp.bfloat16)
-    output = stream + 0.5 * (
-        forward_dot(active, weights[prefix + "_w_out"]) + vector(weights, prefix + "_b_out")
-    )
-    return (output, (normed_b, hidden, active))
-
-
-def ffn_backward(stream, weights, prefix, stored, grad_out):
-    normed_b, hidden, active = stored
-    half_grad = 0.5 * grad_out
-    half_b = half_grad.astype(jnp.bfloat16)
-    gradients = {
-        prefix + "_w_out": (active, half_b),
-        prefix + "_b_out": jnp.sum(half_grad, 0),
-    }
-    d_hidden = back_dot(half_b, weights[prefix + "_w_out"]) * swish_grad(hidden)
-    d_hidden_b = d_hidden.astype(jnp.bfloat16)
-    gradients[prefix + "_w_in"] = (normed_b, d_hidden_b)
-    gradients[prefix + "_b_in"] = jnp.sum(d_hidden, 0)
-    d_normed = back_dot(d_hidden_b, weights[prefix + "_w_in"])
-    d_stream, gain_grad, shift_grad = norm_back(
-        stream,
-        vector(weights, prefix + "_ng"),
-        vector(weights, prefix + "_nb"),
-        d_normed,
-    )
-    gradients[prefix + "_ng"] = gain_grad
-    gradients[prefix + "_nb"] = shift_grad
-    return (grad_out + d_stream, gradients)
 
 
 MESH = pl.DeviceIdType.MESH
@@ -511,23 +445,21 @@
     )(g)
 
 
-def weight_kernel(plan, names, *refs):
-    inputs = dict(zip(names, refs))
-    out, mix = refs[len(names) :]
+def weight_kernel(plan, names, places, *refs):
+    pairs = {name: refs[2 * i : 2 * i + 2] for i, name in enumerate(names)}
+    vectors = refs[2 * len(names) : -2]
+    out, mix = refs[-2:]
     rows = (((0,), (0,)), ((), ()))
     for name, shape in segments():
         first = plan.places[name]
         if math.prod(shape) < D * D:
-            values = inputs[name + "0"]
+            array, begin = places[name]
             for r in range(-(-math.prod(shape) // LANES)):
-                if name == "w_depth":
-                    line = inputs[name + str(r)][...]
-                else:
-                    line = values[:, r * LANES : (r + 1) * LANES]
+                line = vectors[array][begin + r : begin + r + 1, :]
                 tile, row = divmod(first + r, 8)
                 out[tile, row : row + 1, : line.shape[1]] = line.astype(out.dtype)
             continue
-        left, right = inputs[name + "0"], inputs[name + "1"]
+        left, right = pairs[name]
         fold = shape[1] // LANES
         step = 256 if fold == 1 else 128
 
@@ -545,96 +477,18 @@
             out[pl.ds(first // 8 + i * tiles, tiles)] = value.astype(out.dtype).reshape(tiles, 8, LANES)
 
 
-def weight_grads(plan, gradients):
-    names, operands = [], []
-    for name, shape in segments():
-        extent = math.prod(shape)
-        if extent >= D * D:
-            parts = gradients[name]
-        elif name == "w_depth":
-            parts = [value.reshape(1, D) for value in gradients[name]]
-        else:
-            parts = [gradients[name].reshape(1, extent)]
-        for number, value in enumerate(parts):
-            names.append(name + str(number))
-            operands.append(value)
-    vmem = pl.BlockSpec(memory_space=pltpu.VMEM)
+def weight_grads(plan, gradients, vectors, places):
+    names = list(gradients)
+    operands = [value for name in names for value in gradients[name]] + vectors
     return pl.pallas_call(
-        functools.partial(weight_kernel, plan, names),
+        functools.partial(weight_kernel, plan, names, places),
         out_shape=jax.ShapeDtypeStruct((plan.padded, 8, LANES), jnp.bfloat16),
-        in_specs=[vmem] * len(operands),
-        out_specs=vmem,
+        in_specs=[VMEM_SPEC] * len(operands),
+        out_specs=VMEM_SPEC,
         scratch_shapes=[pltpu.VMEM((LANES // 128, 512, 128), jnp.float32)],
         compiler_params=pltpu.CompilerParams(vmem_limit_bytes=60 * 1024 * 1024),
         name="weight_grads",
     )(*operands)
-
-
-def sum_kernel(ndp, nseq, left, right, valid, out, part, line, cross, seq_send, seq_recv, dp_send, dp_recv):
-    di, z = lax.axis_index(DP), lax.axis_index(SEQ)
-    barrier = pltpu.get_barrier_semaphore()
-    peers = [(di, lax.rem(z + i, nseq)) for i in range(1, nseq)]
-    peers = peers + [(lax.rem(di + i, ndp), z) for i in range(1, ndp)]
-    for peer in peers:
-        pl.semaphore_signal(barrier, inc=1, device_id=peer, device_id_type=MESH)
-    value, mask = left[...], valid[...]
-    value = value * mask
-    rows = [
-        jnp.sum(value, 0, keepdims=True),
-        jnp.sum(value * right[...], 0, keepdims=True),
-        jnp.broadcast_to(jnp.sum(mask, 0, keepdims=True), (1, LANES)),
-        jnp.zeros((5, LANES), jnp.float32),
-    ]
-    part[...] = jnp.concatenate(rows, 0)
-    pl.semaphore_wait(barrier, len(peers))
-
-    def exchange(count, me, target, slots, send, recv):
-        copies = []
-        for i in range(1, count):
-            copy = pltpu.make_async_remote_copy(
-                src_ref=part, dst_ref=slots.at[me], send_sem=send.at[i], recv_sem=recv.at[me],
-                device_id=target(lax.rem(me + i, count)), device_id_type=MESH,
-            )
-            copy.start()
-            copies.append(copy)
-        slots[me] = part[...]
-        for i in range(1, count):
-            source = lax.rem(me + count - i, count)
-            pltpu.make_async_remote_copy(
-                src_ref=part, dst_ref=slots.at[source], send_sem=send.at[i], recv_sem=recv.at[source],
-                device_id=(di, z), device_id_type=MESH,
-            ).wait_recv()
-        for copy in copies:
-            copy.wait_send()
-        total = slots[0]
-        for i in range(1, count):
-            total = total + slots[i]
-        return total
-
-    part[...] = exchange(nseq, z, lambda i: (di, i), line, seq_send, seq_recv)
-    out[...] = exchange(ndp, di, lambda i: (i, z), cross, dp_send, dp_recv)
-
-
-def batch_sums(left, right, valid, number):
-    ndp, nseq = lax.axis_size(DP), lax.axis_size(SEQ)
-    vmem = pl.BlockSpec(memory_space=pltpu.VMEM)
-    return pl.pallas_call(
-        functools.partial(sum_kernel, ndp, nseq),
-        out_shape=jax.ShapeDtypeStruct((8, LANES), jnp.float32),
-        in_specs=[vmem] * 3,
-        out_specs=vmem,
-        scratch_shapes=[
-            pltpu.VMEM((8, LANES), jnp.float32),
-            pltpu.VMEM((nseq, 8, LANES), jnp.float32),
-            pltpu.VMEM((ndp, 8, LANES), jnp.float32),
-            pltpu.SemaphoreType.DMA((nseq,)),
-            pltpu.SemaphoreType.DMA((nseq,)),
-            pltpu.SemaphoreType.DMA((ndp,)),
-            pltpu.SemaphoreType.DMA((ndp,)),
-        ],
-        compiler_params=pltpu.CompilerParams(collective_id=number, has_side_effects=True),
-        name="batch_sums" + str(number),
-    )(left, right, valid)
 
 
 def bucket_window(rel_bucket, block_len, full_len):
@@ -786,19 +640,11 @@
     return lax.psum_scatter(rows, SEQ, scatter_dimension=1, tiled=True)
 
 
-def attend_forward(stream, weights, lengths, onehot, seq_count):
-    normed_b = norm_rows(
-        stream, vector(weights, "attn_ng"), vector(weights, "attn_nb")
-    ).astype(jnp.bfloat16)
+def attend_forward(normed_b, queries, weights, lengths, onehot, seq_count):
     normed_all = seq_gather(normed_b, seq_count)
-    queries = (forward_dot(normed_b, weights["w_q"]) + vector(weights, "b_q")).astype(
-        jnp.bfloat16
-    )
     flat_all = normed_all.reshape(-1, D)
     keys = forward_dot(flat_all, weights["w_k"]).astype(jnp.bfloat16)
-    values = (forward_dot(flat_all, weights["w_v"]) + vector(weights, "b_v")).astype(
-        jnp.bfloat16
-    )
+    values = (forward_dot(flat_all, weights["w_v"]) + vector(weights, "b_v")).astype(jnp.bfloat16)
     table = lax.dot_general(
         weights["rel"], onehot.astype(jnp.bfloat16), (((0,), (1,)), ((), ())),
         preferred_element_type=jnp.float32,
@@ -807,119 +653,19 @@
     keys3 = keys.reshape(seq_count, -1, D)
     values3 = values.reshape(seq_count, -1, D)
     context, lse = attend(lengths, queries3, keys3, values3, table)
-    context = context.reshape(-1, D)
-    output = stream + forward_dot(context, weights["w_o"]) + vector(weights, "b_o")
-    return (output, (normed_b, flat_all, queries3, keys3, values3, table, lse, context))
-
-
-def attend_backward(stream, weights, stored, grad_out, lengths, onehot):
-    normed_b, flat_all, queries3, keys3, values3, table, lse, context = stored
-    grad_b = grad_out.astype(jnp.bfloat16)
-    gradients = {"w_o": (context, grad_b), "b_o": jnp.sum(grad_out, 0)}
-    d_context = back_dot(grad_b, weights["w_o"]).astype(jnp.bfloat16).reshape(queries3.shape)
+    return context.reshape(-1, D), (flat_all, queries3, keys3, values3, table, lse)
+
+
+def attend_backward(weights, stored, d_context, lengths, onehot):
+    flat_all, queries3, keys3, values3, table, lse = stored
+    d_context = d_context.reshape(queries3.shape)
     dq, dk, dv, dt, sums = attend_back(lengths, queries3, keys3, values3, table, lse, d_context)
-    gradients["rel"] = lax.dot_general(
-        onehot, dt, (((0,), (1,)), ((), ())), precision=lax.Precision.HIGHEST
-    )
+    rel_grad = lax.dot_general(onehot, dt, (((0,), (1,)), ((), ())), precision=lax.Precision.HIGHEST)
     query_b, key_b, value_b = dq.reshape(-1, D), dk.reshape(-1, D), dv.reshape(-1, D)
     remote = back_dot(key_b, weights["w_k"]) + back_dot(value_b, weights["w_v"])
-    remote = seq_scatter(remote.astype(jnp.bfloat16).reshape(keys3.shape)).reshape(stream.shape)
-    gradients["w_q"] = (normed_b, query_b)
-    gradients["b_q"] = sums[0]
-    gradients["w_k"] = (flat_all, key_b)
-    gradients["w_v"] = (flat_all, value_b)
-    gradients["b_v"] = sums[1]
-    d_normed = back_dot(query_b, weights["w_q"]) + remote.astype(jnp.float32)
-    d_stream, gain_grad, shift_grad = norm_back(
-        stream, vector(weights, "attn_ng"), vector(weights, "attn_nb"), d_normed
-    )
-    gradients["attn_ng"] = gain_grad
-    gradients["attn_nb"] = shift_grad
-    return (grad_out + d_stream, gradients)
-
-
-def depthwise(padded, kernel):
-    length = padded.shape[1] - kernel.shape[0] + 1
-    summed = jnp.zeros((padded.shape[0], length, padded.shape[2]), jnp.float32)
-    for offset in range(kernel.shape[0]):
-        summed = summed + kernel[offset] * padded[:, offset : offset + length]
-    return summed.reshape(-1, padded.shape[2])
-
-
-def depth_back(padded, d_depth3, d_padded, kernel):
-    length = d_depth3.shape[1]
-    taps_count = kernel.shape[0]
-    kernel_grad = [
-        jnp.sum(padded[:, offset : offset + length] * d_depth3, (0, 1))
-        for offset in range(taps_count)
-    ]
-    d_gated = jnp.zeros(d_depth3.shape, jnp.float32)
-    for offset in range(taps_count):
-        start_at = taps_count - 1 - offset
-        d_gated = d_gated + kernel[offset] * d_padded[:, start_at : start_at + length]
-    return (kernel_grad, d_gated.reshape(-1, d_depth3.shape[2]))
-
-
-def conv_front(stream, weights, valid_rows, seq_count):
-    normed_b = norm_rows(
-        stream, vector(weights, "conv_ng"), vector(weights, "conv_nb")
-    ).astype(jnp.bfloat16)
-    pre_gate = forward_dot(normed_b, weights["w_pi"]) + vector(weights, "b_pi")
-    gated = pre_gate[:, :D] * jax.nn.sigmoid(pre_gate[:, D:]) * valid_rows[:, None]
-    padded = with_halo(gated.reshape(seq_count, -1, D), ((SEQ, 1),), K // 2)
-    depth = depthwise(padded, vector(weights, "w_depth"))
-    return (normed_b, pre_gate, padded, depth)
-
-
-def conv_tail(stream, weights, depth, batch_mean, inv_std):
-    standard = (depth - batch_mean) * inv_std
-    normed_bn = standard * vector(weights, "bng") + vector(weights, "bnb")
-    active = swish_act(normed_bn).astype(jnp.bfloat16)
-    output = stream + forward_dot(active, weights["w_po"]) + vector(weights, "b_po")
-    return (output, (standard, normed_bn, active))
-
-
-def conv_tail_back(weights, stored, grad_out, valid_rows):
-    standard, normed_bn, active = stored
-    grad_b = grad_out.astype(jnp.bfloat16)
-    gradients = {"w_po": (active, grad_b), "b_po": jnp.sum(grad_out, 0)}
-    d_normed = back_dot(grad_b, weights["w_po"]) * swish_grad(normed_bn)
-    gradients["bng"] = jnp.sum(d_normed * standard, 0)
-    gradients["bnb"] = jnp.sum(d_normed, 0)
-    d_standard = d_normed * vector(weights, "bng") * valid_rows[:, None]
-    return (d_standard, gradients)
-
-
-def gate_back(stream, weights, normed_b, pre_gate, d_gated, valid_rows, grad_out, kernel_grad):
-    linear_half = pre_gate[:, :D]
-    gate_sig = jax.nn.sigmoid(pre_gate[:, D:])
-    d_gated = d_gated * valid_rows[:, None]
-    d_pre = jnp.concatenate(
-        [d_gated * gate_sig, d_gated * linear_half * gate_sig * (1.0 - gate_sig)], 1
-    )
-    d_pre_b = d_pre.astype(jnp.bfloat16)
-    gradients = {
-        "w_depth": kernel_grad,
-        "w_pi": (normed_b, d_pre_b),
-        "b_pi": jnp.sum(d_pre, 0),
-    }
-    d_normed = back_dot(d_pre_b, weights["w_pi"])
-    d_stream, gain_grad, shift_grad = norm_back(
-        stream, vector(weights, "conv_ng"), vector(weights, "conv_nb"), d_normed
-    )
-    gradients["conv_ng"] = gain_grad
-    gradients["conv_nb"] = shift_grad
-    return (grad_out + d_stream, gradients)
-
-
-def conv_front_back(stream, weights, stored, d_depth, valid_rows, grad_out, seq_count):
-    normed_b, pre_gate, padded, depth = stored
-    d_depth3 = d_depth.reshape(seq_count, -1, D)
-    d_padded = with_halo(d_depth3, ((SEQ, 1),), K // 2)
-    kernel_grad, d_gated = depth_back(padded, d_depth3, d_padded, vector(weights, "w_depth"))
-    return gate_back(
-        stream, weights, normed_b, pre_gate, d_gated, valid_rows, grad_out, kernel_grad
-    )
+    remote = seq_scatter(remote.astype(jnp.bfloat16).reshape(keys3.shape)).reshape(query_b.shape)
+    gradients = {"w_k": (flat_all, key_b), "w_v": (flat_all, value_b)}
+    return query_b, remote, rel_grad.reshape(1, -1), sums, gradients
 
 
 def adam_update(param_vec, grad_in, first_mom, second):
@@ -931,58 +677,521 @@
     return (param_vec - LEARN_RATE * (step_size + DECAY * param_vec), new_first, new_second)
 
 
+def unit_rows(values):
+    centre = values - jnp.mean(values, -1, keepdims=True)
+    scale = lax.rsqrt(jnp.mean(centre * centre, -1, keepdims=True) + NORM_EPS)
+    return centre * scale, scale
+
+
+def unit_back(unit, scale, gain, grad):
+    shifted = grad * gain
+    first = jnp.mean(shifted, -1, keepdims=True)
+    second = jnp.mean(shifted * unit, -1, keepdims=True)
+    return scale * (shifted - first - unit * second), total_rows(grad * unit), total_rows(grad)
+
+
+def total_rows(values):
+    return jnp.sum(values, 0, keepdims=True)
+
+
+def split_rows(source, mix, target, fold):
+    block = mix.shape[1]
+    lanes = LANES // 128
+
+    @pl.loop(0, source.shape[0] // block)
+    def _(i):
+        part = source[pl.ds(pl.multiple_of(i * block, block), block), :].astype(jnp.float32)
+        for lane in range(lanes):
+            mix[lane] = part[:, lane * 128 : (lane + 1) * 128]
+        for j in range(fold):
+            rows = [mix[lane, pl.ds(j, block // fold, stride=fold), :] for lane in range(lanes)]
+            at = pl.multiple_of(i * (block // fold), block // fold)
+            target[j, pl.ds(at, block // fold), :] = jnp.concatenate(rows, 1).astype(target.dtype)
+
+
+class Fetch:
+    def __init__(self, plan, packed, sem):
+        self.plan, self.packed, self.sem, self.count = plan, packed, sem, 0
+
+    def __call__(self, name, target):
+        row = self.plan.places[name] // 8 * 8
+        copy = pltpu.make_async_copy(
+            self.packed.at[pl.ds(row, target.shape[0])], target, self.sem.at[self.count]
+        )
+        self.count += 1
+        copy.start()
+        return copy
+
+
+def wait_all(*copies):
+    for copy in copies:
+        copy.wait()
+
+
+def ffn_first_kernel(plan, x, packed, x_out, n_out, q_out, w_out, w_in, w_second, w_q, v0, v1, v2, v3, mix, sem):
+    fetch = Fetch(plan, packed, sem)
+    early = [fetch("first_ng", v0), fetch("first_b_in", v1), fetch("first_b_out", v2), fetch("b_q", v3)]
+    in_copy = fetch("first_w_in", w_in)
+    late = [fetch("first_w_out", w_second), fetch("w_q", w_q)]
+    wait_all(*early)
+    gains, bias_in, tail = v0[...].astype(jnp.float32), v1[...].astype(jnp.float32), v2[...].astype(jnp.float32)
+    stream = x[...]
+    unit, _ = unit_rows(stream)
+    normed = (unit * gains[0:1] + gains[1:2]).astype(jnp.bfloat16)
+    in_copy.wait()
+    split_rows(w_in, mix, w_out, FF // LANES)
+    wait_all(*late)
+    total = jnp.zeros(stream.shape, jnp.float32)
+    for j in range(FF // LANES):
+        hidden = forward_dot(normed, w_out[j]) + bias_in[j : j + 1]
+        active = swish_act(hidden).astype(jnp.bfloat16)
+        total = total + forward_dot(active, w_second[j * LANES : (j + 1) * LANES, :])
+    stream = stream + 0.5 * (total + tail[0:1])
+    x_out[...] = stream
+    unit, _ = unit_rows(stream)
+    normed = (unit * tail[1:2] + tail[2:3]).astype(jnp.bfloat16)
+    n_out[...] = normed
+    q_out[...] = (forward_dot(normed, w_q[...]) + v3[...].astype(jnp.float32)[0:1]).astype(jnp.bfloat16)
+
+
+def ffn_first_back_kernel(plan, x, x_one, d_two, d_query, remote, w_in, packed,
+                          d_out, a_out, r_out, n_out, h_out, vec_out, w_second, w_q, v0, v1, v2, sem):
+    fetch = Fetch(plan, packed, sem)
+    early = [fetch("first_ng", v0), fetch("first_b_in", v1), fetch("first_b_out", v2), fetch("w_q", w_q)]
+    late = fetch("first_w_out", w_second)
+    wait_all(*early)
+    gains, bias_in, tail = v0[...].astype(jnp.float32), v1[...].astype(jnp.float32), v2[...].astype(jnp.float32)
+    unit, scale = unit_rows(x_one[...])
+    d_normed = back_dot(d_query[...], w_q[...]) + remote[...].astype(jnp.float32)
+    d_norm, gain_grad, shift_grad = unit_back(unit, scale, tail[1:2], d_normed)
+    vec_out[0:1] = gain_grad
+    vec_out[1:2] = shift_grad
+    grad = d_two[...] + d_norm
+    half = 0.5 * grad
+    vec_out[2:3] = total_rows(half)
+    half_b = half.astype(jnp.bfloat16)
+    r_out[...] = half_b
+    unit, scale = unit_rows(x[...])
+    normed = (unit * gains[0:1] + gains[1:2]).astype(jnp.bfloat16)
+    n_out[...] = normed
+    late.wait()
+    d_normed = jnp.zeros(grad.shape, jnp.float32)
+    for j in range(FF // LANES):
+        cols = slice(j * LANES, (j + 1) * LANES)
+        hidden = forward_dot(normed, w_in[j]) + bias_in[j : j + 1]
+        a_out[:, cols] = swish_act(hidden).astype(jnp.bfloat16)
+        d_hidden = back_dot(half_b, w_second[cols, :]) * swish_grad(hidden)
+        vec_out[5 + j : 6 + j] = total_rows(d_hidden)
+        d_hidden = d_hidden.astype(jnp.bfloat16)
+        h_out[:, cols] = d_hidden
+        d_normed = d_normed + back_dot(d_hidden, w_in[j])
+    d_norm, gain_grad, shift_grad = unit_back(unit, scale, gains[0:1], d_normed)
+    vec_out[3:4] = gain_grad
+    vec_out[4:5] = shift_grad
+    d_out[...] = grad + d_norm
+
+
+def gate_kernel(plan, ctx, x, valid, packed, x_out, n_out, g_out, u_out, w_out, w_o, w_pi, v0, v1, mix, sem):
+    fetch = Fetch(plan, packed, sem)
+    early = [fetch("w_o", w_o), fetch("b_o", v0), fetch("b_pi", v1)]
+    late = fetch("w_pi", w_pi)
+    wait_all(*early)
+    rows, bias_in = v0[...].astype(jnp.float32), v1[...].astype(jnp.float32)
+    stream = x[...] + forward_dot(ctx[...], w_o[...]) + rows[0:1]
+    x_out[...] = stream
+    unit, _ = unit_rows(stream)
+    normed = (unit * rows[6:7] + rows[7:8]).astype(jnp.bfloat16)
+    n_out[...] = normed
+    late.wait()
+    split_rows(w_pi, mix, w_out, 2)
+    linear = forward_dot(normed, w_out[0]) + bias_in[0:1]
+    gate = forward_dot(normed, w_out[1]) + bias_in[1:2]
+    g_out[:, :D] = linear
+    g_out[:, D:] = gate
+    u_out[...] = linear * jax.nn.sigmoid(gate) * valid[...]
+
+
+def gate_back_kernel(plan, du, pre_gate, x, d_three, valid, w_pi, packed,
+                     g_out, d_out, o_out, c_out, vec_out, w_o, v0, sem):
+    fetch = Fetch(plan, packed, sem)
+    copies = [fetch("b_o", v0), fetch("w_o", w_o)]
+    d_gated = du[...] * valid[...]
+    gate_sig = jax.nn.sigmoid(pre_gate[:, D:])
+    d_linear = d_gated * gate_sig
+    d_gate = d_gated * pre_gate[:, :D] * gate_sig * (1.0 - gate_sig)
+    vec_out[0:1] = total_rows(d_linear)
+    vec_out[1:2] = total_rows(d_gate)
+    d_linear, d_gate = d_linear.astype(jnp.bfloat16), d_gate.astype(jnp.bfloat16)
+    g_out[:, :D] = d_linear
+    g_out[:, D:] = d_gate
+    d_normed = back_dot(d_linear, w_pi[0]) + back_dot(d_gate, w_pi[1])
+    unit, scale = unit_rows(x[...])
+    wait_all(*copies)
+    d_norm, gain_grad, shift_grad = unit_back(unit, scale, v0[...].astype(jnp.float32)[6:7], d_normed)
+    vec_out[2:3] = gain_grad
+    vec_out[3:4] = shift_grad
+    grad = d_three[...] + d_norm
+    d_out[...] = grad
+    vec_out[4:5] = total_rows(grad)
+    grad_b = grad.astype(jnp.bfloat16)
+    o_out[...] = grad_b
+    c_out[...] = back_dot(grad_b, w_o[...]).astype(jnp.bfloat16)
+
+
+def middle_kernel(plan, x, depth, sums, cot, valid, packed,
+                  y_out, d_out, z_out, part_out, stat_out, e_out, rb_out, a_out, r_out, n_out, h_out, vec_out,
+                  w_po, w_in, w_second, w_mix, held, v_bn, v0, v1, v2, mix, sem):
+    fetch = Fetch(plan, packed, sem)
+    early = [fetch("b_pi", v_bn), fetch("w_po", w_po), fetch("b_po", v0), fetch("second_b_in", v1)]
+    early.append(fetch("second_b_out", v2))
+    in_copy = fetch("second_w_in", w_in)
+    late = fetch("second_w_out", w_second)
+    wait_all(*early)
+    base = plan.places["bng"] - plan.places["b_pi"]
+    batch, head = v_bn[...].astype(jnp.float32), v0[...].astype(jnp.float32)
+    bias_in, tail = v1[...].astype(jnp.float32), v2[...].astype(jnp.float32)
+    gain, shift = batch[base : base + 1], batch[base + 1 : base + 2]
+    count = sums[2:3]
+    mean = sums[0:1] / count
+    inv_std = lax.rsqrt(sums[1:2] / count - mean * mean + BATCH_EPS)
+    stat_out[0:1] = mean
+    stat_out[1:2] = inv_std
+    stat_out[2:3] = count
+    stat_out[3:8] = jnp.zeros((5, D), jnp.float32)
+    standard = (depth[...] - mean) * inv_std
+    e_out[...] = swish_act(standard * gain + shift).astype(jnp.bfloat16)
+    three = x[...] + forward_dot(e_out[...], w_po[...]) + head[0:1]
+    unit, scale = unit_rows(three)
+    n_out[...] = (unit * head[1:2] + head[2:3]).astype(jnp.bfloat16)
+    in_copy.wait()
+    split_rows(w_in, mix, w_mix, FF // LANES)
+    late.wait()
+    total = jnp.zeros(three.shape, jnp.float32)
+    for j in range(FF // LANES):
+        cols = slice(j * LANES, (j + 1) * LANES)
+        hidden = forward_dot(n_out[...], w_mix[j]) + bias_in[j : j + 1]
+        held[j] = hidden
+        active = swish_act(hidden).astype(jnp.bfloat16)
+        a_out[:, cols] = active
+        total = total + forward_dot(active, w_second[cols, :])
+    four = three + 0.5 * (total + tail[0:1])
+    last, last_scale = unit_rows(four)
+    y_out[...] = last * tail[1:2] + tail[2:3]
+    grad = cot[...] * valid[...]
+    grad, gain_grad, shift_grad = unit_back(last, last_scale, tail[1:2], grad)
+    vec_out[0:1] = gain_grad
+    vec_out[1:2] = shift_grad
+    half = 0.5 * grad
+    vec_out[2:3] = total_rows(half)
+    r_out[...] = half.astype(jnp.bfloat16)
+    d_normed = jnp.zeros(three.shape, jnp.float32)
+    for j in range(FF // LANES):
+        cols = slice(j * LANES, (j + 1) * LANES)
+        d_hidden = back_dot(r_out[...], w_second[cols, :]) * swish_grad(held[j])
+        vec_out[8 + j : 9 + j] = total_rows(d_hidden)
+        d_hidden = d_hidden.astype(jnp.bfloat16)
+        h_out[:, cols] = d_hidden
+        d_normed = d_normed + back_dot(d_hidden, w_mix[j])
+    d_norm, gain_grad, shift_grad = unit_back(unit, scale, head[1:2], d_normed)
+    vec_out[3:4] = gain_grad
+    vec_out[4:5] = shift_grad
+    grad = grad + d_norm
+    d_out[...] = grad
+    vec_out[5:6] = total_rows(grad)
+    rb_out[...] = grad.astype(jnp.bfloat16)
+    standard = (depth[...] - mean) * inv_std
+    d_active = back_dot(rb_out[...], w_po[...]) * swish_grad(standard * gain + shift)
+    d_gain, d_shift = total_rows(d_active * standard), total_rows(d_active)
+    vec_out[6:7] = d_gain
+    vec_out[7:8] = d_shift
+    vec_out[12:16] = jnp.zeros((4, D), jnp.float32)
+    d_standard = d_active * gain * valid[...]
+    z_out[...] = d_standard
+    part_out[0:1] = total_rows(d_standard)
+    part_out[1:2] = total_rows(d_standard * standard)
+    part_out[2:8] = jnp.zeros((6, D), jnp.float32)
+
+
+def group_barrier(ndp, nseq):
+    di, z = lax.axis_index(DP), lax.axis_index(SEQ)
+    peers = [(di, lax.rem(z + i, nseq)) for i in range(1, nseq)]
+    peers = peers + [(lax.rem(di + i, ndp), z) for i in range(1, ndp)]
+    barrier = pltpu.get_barrier_semaphore()
+    for peer in peers:
+        pl.semaphore_signal(barrier, inc=1, device_id=peer, device_id_type=MESH)
+    return lambda: pl.semaphore_wait(barrier, len(peers))
+
+
+def exchange_sum(ndp, nseq, part, line, cross, sems):
+    di, z = lax.axis_index(DP), lax.axis_index(SEQ)
+
+    def phase(count, me, target, slots, send, recv):
+        copies = []
+        for i in range(1, count):
+            copy = pltpu.make_async_remote_copy(
+                src_ref=part, dst_ref=slots.at[me], send_sem=send.at[i], recv_sem=recv.at[me],
+                device_id=target(lax.rem(me + i, count)), device_id_type=MESH,
+            )
+            copy.start()
+            copies.append(copy)
+        slots[me] = part[...]
+        for i in range(1, count):
+            source = lax.rem(me + count - i, count)
+            pltpu.make_async_remote_copy(
+                src_ref=part, dst_ref=slots.at[source], send_sem=send.at[i], recv_sem=recv.at[source],
+                device_id=(di, z), device_id_type=MESH,
+            ).wait_recv()
+        for copy in copies:
+            copy.wait_send()
+        total = slots[0]
+        for i in range(1, count):
+            total = total + slots[i]
+        return total
+
+    part[...] = phase(nseq, z, lambda i: (di, i), line, sems[0], sems[1])
+    return phase(ndp, di, lambda i: (i, z), cross, sems[2], sems[3])
+
+
+HALO = 16
+
+
+class Halo:
+    def __init__(self, nseq, buffer, sem):
+        di, z = lax.axis_index(DP), lax.axis_index(SEQ)
+        rows = buffer.shape[1]
+        self.has = (z > 0, z < nseq - 1)
+
+        def copy(source, target, number, to):
+            return pltpu.make_async_remote_copy(
+                src_ref=buffer.at[:, pl.ds(source, HALO)], dst_ref=buffer.at[:, pl.ds(target, HALO)],
+                send_sem=sem.at[number], recv_sem=sem.at[2 + number], device_id=(di, to), device_id_type=MESH,
+            )
+
+        self.up = copy(rows - 2 * HALO, 0, 0, lax.rem(z + 1, nseq))
+        self.down = copy(HALO, rows - HALO, 1, lax.rem(z + nseq - 1, nseq))
+        self.buffer, self.rows = buffer, rows
+
+    def start(self):
+        @pl.when(self.has[1])
+        def _():
+            self.up.start()
+
+        @pl.when(self.has[0])
+        def _():
+            self.down.start()
+
+    def finish(self):
+        empty = jnp.zeros((self.buffer.shape[0], HALO, self.buffer.shape[2]), jnp.float32)
+
+        @pl.when(self.has[0])
+        def _():
+            self.up.wait_recv()
+            self.down.wait_send()
+
+        @pl.when(jnp.logical_not(self.has[0]))
+        def _():
+            self.buffer[:, :HALO] = empty
+
+        @pl.when(self.has[1])
+        def _():
+            self.down.wait_recv()
+            self.up.wait_send()
+
+        @pl.when(jnp.logical_not(self.has[1]))
+        def _():
+            self.buffer[:, self.rows - HALO :] = empty
+
+
+def slide(padded, taps, index, out, length):
+    lanes = LANES // 128
+
+    @pl.loop(0, padded.shape[0] * lanes)
+    def _(i):
+        s, lane = i // lanes, pl.ds(pl.multiple_of(i % lanes * 128, 128), 128)
+        total = jnp.zeros((length, 128), jnp.float32)
+        for b in range(8):
+            part = None
+            for a in range(4):
+                if 0 < 8 * a + b < K + 1:
+                    row = index(8 * a + b)
+                    term = taps[row : row + 1, lane] * padded[s, 8 * a : 8 * a + length + 8, lane]
+                    part = term if part is None else part + term
+            total = total + part[b : b + length]
+        out[pl.ds(pl.multiple_of(s * length, length), length), lane] = total
+
+
+def depth_kernel(plan, u, valid, packed, c_out, sum_out, padded, taps, taps_b, part, line, cross, sem,
+                 halo_sem, *sems):
+    ndp, nseq = plan.ndp, plan.nseq
+    arrived = group_barrier(ndp, nseq)
+    length = padded.shape[1] - 2 * HALO
+    copy = Fetch(plan, packed, sem)("b_pi", taps_b)
+    padded[:, HALO : HALO + length] = u[...].reshape(-1, length, D)
+    arrived()
+    halo = Halo(nseq, padded, halo_sem)
+    halo.start()
+    copy.wait()
+    taps[...] = taps_b[...].astype(jnp.float32)
+    halo.finish()
+    base = plan.places["w_depth"] - plan.places["b_pi"]
+    slide(padded, taps, lambda i: base + i - 1, c_out, length)
+    depth, mask = c_out[...], valid[...]
+    value = depth * mask
+    part[0:1] = total_rows(value)
+    part[1:2] = total_rows(value * depth)
+    part[2:3] = jnp.broadcast_to(total_rows(mask), (1, LANES))
+    part[3:8] = jnp.zeros((5, LANES), jnp.float32)
+    sum_out[...] = exchange_sum(ndp, nseq, part, line, cross, sems)
+
+
+def depth_back_kernel(plan, dz, depth, stats, local, valid, u_pad, packed, u_out, tap_out,
+                      padded, own, taps, taps_b, part, line, cross, sem, halo_sem, *sems):
+    ndp, nseq = plan.ndp, plan.nseq
+    arrived = group_barrier(ndp, nseq)
+    seqs, length = padded.shape[0], padded.shape[1] - 2 * HALO
+    copy = Fetch(plan, packed, sem)("b_pi", taps_b)
+    part[...] = local[...]
+    arrived()
+    sums = exchange_sum(ndp, nseq, part, line, cross, sems)
+    mean, inv_std, count = stats[0:1], stats[1:2], stats[2:3]
+    standard = (depth[...] - mean) * inv_std
+    d_depth = valid[...] * inv_std * (dz[...] - sums[0:1] / count - standard * (sums[1:2] / count))
+    d_depth = d_depth.reshape(seqs, length, D)
+    padded[:, HALO : HALO + length] = d_depth
+    halo = Halo(nseq, padded, halo_sem)
+    halo.start()
+    own[:, :8] = jnp.zeros((seqs, 8, D), jnp.float32)
+    own[:, 8 : 8 + length] = d_depth
+    own[:, 8 + length :] = jnp.zeros((seqs, 8, D), jnp.float32)
+    copy.wait()
+    taps[...] = taps_b[...].astype(jnp.float32)
+    base = plan.places["w_depth"] - plan.places["b_pi"]
+
+    @pl.loop(0, LANES // 128)
+    def _(i):
+        lane = pl.ds(pl.multiple_of(i * 128, 128), 128)
+        for b in range(8):
+            sums_b = [None] * 4
+            for s in range(seqs):
+                moved = own[s, 8 - b : 8 - b + length + 8, lane]
+                for a in range(4):
+                    if 0 < 8 * a + b < K + 1:
+                        term = total_rows(u_pad[s, 8 * a : 8 * a + length + 8, lane] * moved)
+                        sums_b[a] = term if sums_b[a] is None else sums_b[a] + term
+            for a in range(4):
+                if sums_b[a] is not None:
+                    tap_out[8 * a + b - 1 : 8 * a + b, lane] = sums_b[a]
+        tap_out[K : K + 1, lane] = jnp.zeros((1, 128), jnp.float32)
+
+    halo.finish()
+    slide(padded, taps, lambda i: base + K - i, u_out, length)
+
+
+VMEM_SPEC = pl.BlockSpec(memory_space=pltpu.VMEM)
+ANY_SPEC = pl.BlockSpec(memory_space=pl.ANY)
+
+
+def stage(kernel, plan, operands, packed, outs, scratch, name, number=None):
+    params = {}
+    if number is not None:
+        params = {"collective_id": number, "has_side_effects": True}
+    specs = [VMEM_SPEC] * len(operands) + [ANY_SPEC]
+    return pl.pallas_call(
+        functools.partial(kernel, plan),
+        out_shape=[jax.ShapeDtypeStruct(shape, dtype) for shape, dtype in outs],
+        in_specs=specs,
+        out_specs=[VMEM_SPEC] * len(outs),
+        scratch_shapes=scratch,
+        compiler_params=pltpu.CompilerParams(vmem_limit_bytes=56 * 1024 * 1024, **params),
+        name=name,
+    )(*operands, packed)
+
+
+F32, BF16 = jnp.float32, jnp.bfloat16
+DMA = pltpu.SemaphoreType.DMA
+
+
+def vm(shape, dtype=jnp.bfloat16):
+    return pltpu.VMEM(shape, dtype)
+
+
+def exchange_scratch(plan):
+    return [vm((8, D), F32), vm((plan.nseq, 8, D), F32), vm((plan.ndp, 8, D), F32), DMA((1,)), DMA((4,)),
+            DMA((plan.nseq,)), DMA((plan.nseq,)), DMA((plan.ndp,)), DMA((plan.ndp,))]
+
+
 def per_device(inputs, lengths, rel_bucket, params, moment_one, moment_two, cotangent):
     seq_count, block_len, model_width = inputs.shape
+    rows = seq_count * block_len
     full_len = block_len * lax.axis_size(SEQ)
     first_pos = lax.axis_index(SEQ) * block_len
     positions = first_pos + jnp.arange(block_len, dtype=jnp.int32)
     valid_own = positions[None, :] < lengths[:, None]
-    valid_rows = valid_own.astype(jnp.float32).reshape(-1)
+    valid = valid_own.astype(jnp.float32).reshape(-1, 1)
     onehot = bucket_window(rel_bucket, block_len, full_len)
     plan = Plan(lax.axis_size(DP), lax.axis_size(SEQ), params.shape[0])
-    gathered = gather(plan, own_block(plan, params))
-    weights = unpack(gathered.reshape(-1, LANES))
-    stream0 = inputs.reshape(-1, model_width)
-    stream1, stored1 = ffn_forward(stream0, weights, "first")
-    stream2, stored2 = attend_forward(stream1, weights, lengths, onehot, seq_count)
-    stored3 = conv_front(stream2, weights, valid_rows, seq_count)
-    depth = stored3[3]
-    valid_column = valid_rows[:, None]
-    sums = batch_sums(depth, depth, valid_column, 2)
-    first_sum, square_sum, token_count = sums[0], sums[1], sums[2, 0]
-    batch_mean = first_sum / token_count
-    inv_std = lax.rsqrt(square_sum / token_count - batch_mean * batch_mean + BATCH_EPS)
-    stream3, stored4 = conv_tail(stream2, weights, depth, batch_mean, inv_std)
-    stream4, stored5 = ffn_forward(stream3, weights, "second")
-    output = norm_rows(stream4, vector(weights, "fin_g"), vector(weights, "fin_b"))
-    grad_out = cotangent.reshape(-1, model_width) * valid_rows[:, None]
-    d_stream4, gain_grad, shift_grad = norm_back(
-        stream4, vector(weights, "fin_g"), vector(weights, "fin_b"), grad_out
+    packed = gather(plan, own_block(plan, params)).reshape(-1, LANES)
+    full, wide = (rows, D), (rows, FF)
+    square, tall, group = vm((D, D)), vm((FF, D)), vm((8, D))
+    mix = vm((LANES // 128, 256, 128), F32)
+    stream0 = inputs.reshape(full)
+    stream1, normed2, queries, w_first = stage(
+        ffn_first_kernel, plan, [stream0], packed,
+        [(full, F32), (full, BF16), (full, BF16), ((FF // D, D, D), BF16)],
+        [tall, tall, square, group, group, group, group, mix, DMA((7,))], "ffn_first",
     )
-    gradients = {"fin_g": gain_grad, "fin_b": shift_grad}
-    d_stream3, partial_grads = ffn_backward(stream3, weights, "second", stored5, d_stream4)
-    gradients.update(partial_grads)
-    d_standard, partial_grads = conv_tail_back(weights, stored4, d_stream3, valid_rows)
-    gradients.update(partial_grads)
-    standard = stored4[0]
-    sums = batch_sums(d_standard, standard, valid_column, 3)
-    sum_dz, sum_dzz = sums[0], sums[1]
-    d_depth = (
-        valid_rows[:, None]
-        * inv_std
-        * (d_standard - sum_dz / token_count - standard * sum_dzz / token_count)
+    weights = unpack(packed)
+    context, stored2 = attend_forward(normed2, queries, weights, lengths, onehot, seq_count)
+    stream2, normed3, pre_gate, gated, w_gate = stage(
+        gate_kernel, plan, [context, stream1, valid], packed,
+        [(full, F32), (full, BF16), ((rows, 2 * D), F32), (full, F32), ((2, D, D), BF16)],
+        [square, vm((2 * D, D)), group, group, mix, DMA((4,))], "gate",
     )
-    d_stream2, partial_grads = conv_front_back(
-        stream2, weights, stored3, d_depth, valid_rows, d_stream3, seq_count
+    padded_shape = (seq_count, block_len + 2 * HALO, D)
+    depth, sums, padded = stage(
+        depth_kernel, plan, [gated, valid], packed,
+        [(full, F32), ((8, D), F32), (padded_shape, F32)],
+        [vm((40, D), F32), vm((40, D))] + exchange_scratch(plan), "depth", 2,
     )
-    gradients.update(partial_grads)
-    d_stream1, partial_grads = attend_backward(
-        stream1, weights, stored2, d_stream2, lengths, onehot
+    (output, d_stream3, d_standard, local, stats, active3, grad3_b, active4, half4, normed4, d_hidden4,
+     vec_mid) = stage(
+        middle_kernel, plan, [stream2, depth, sums, cotangent.reshape(full), valid], packed,
+        [(full, F32), (full, F32), (full, F32), ((8, D), F32), ((8, D), F32), (full, BF16), (full, BF16),
+         (wide, BF16), (full, BF16), (full, BF16), (wide, BF16), ((16, D), F32)],
+        [square, tall, tall, vm((FF // D, D, D)), vm((FF // D, rows, D), F32), vm((40, D)), group, group, group,
+         mix, DMA((7,))], "middle",
     )
-    gradients.update(partial_grads)
-    d_stream0, partial_grads = ffn_backward(stream0, weights, "first", stored1, d_stream1)
-    gradients.update(partial_grads)
-    window = scatter(plan, weight_grads(plan, gradients))
+    d_gated, tap_grads = stage(
+        depth_back_kernel, plan, [d_standard, depth, stats, local, valid, padded], packed,
+        [(full, F32), ((32, D), F32)],
+        [vm(padded_shape, F32), vm((seq_count, block_len + 16, D), F32), vm((40, D), F32), vm((40, D))]
+        + exchange_scratch(plan), "depth_back", 3,
+    )
+    d_gate, d_stream2, grad2_b, d_context, vec_gate = stage(
+        gate_back_kernel, plan, [d_gated, pre_gate, stream2, d_stream3, valid, w_gate], packed,
+        [((rows, 2 * D), BF16), (full, F32), (full, BF16), (full, BF16), ((8, D), F32)],
+        [square, group, DMA((2,))], "gate_back",
+    )
+    d_query, remote, rel_grad, vec_attend, gradients = attend_backward(weights, stored2, d_context, lengths, onehot)
+    d_stream0, active1, half1, normed1, d_hidden1, vec_first = stage(
+        ffn_first_back_kernel, plan, [stream0, stream1, d_stream2, d_query, remote, w_first], packed,
+        [(full, F32), (wide, BF16), (full, BF16), (full, BF16), (wide, BF16), ((16, D), F32)],
+        [tall, square, group, group, group, DMA((5,))], "ffn_first_back",
+    )
+    gradients.update({
+        "first_w_in": (normed1, d_hidden1), "first_w_out": (active1, half1), "w_q": (normed2, d_query),
+        "w_o": (context, grad2_b), "w_pi": (normed3, d_gate), "w_po": (active3, grad3_b),
+        "second_w_in": (normed4, d_hidden4), "second_w_out": (active4, half4),
+    })
+    places = {
+        "attn_ng": (0, 0), "attn_nb": (0, 1), "first_b_out": (0, 2), "first_ng": (0, 3), "first_nb": (0, 4),
+        "first_b_in": (0, 5), "b_pi": (1, 0), "conv_ng": (1, 2), "conv_nb": (1, 3), "b_o": (1, 4),
+        "fin_g": (2, 0), "fin_b": (2, 1), "second_b_out": (2, 2), "second_ng": (2, 3), "second_nb": (2, 4),
+        "b_po": (2, 5), "bng": (2, 6), "bnb": (2, 7), "second_b_in": (2, 8), "w_depth": (3, 0),
+        "b_q": (4, 0), "b_v": (4, 1), "rel": (5, 0),
+    }
+    vectors = [vec_first, vec_gate, vec_mid, tap_grads, vec_attend, rel_grad]
+    window = scatter(plan, weight_grads(plan, gradients, vectors, places))
     grad_shard = own_shard(plan, window)
     new_params, new_first, new_second = adam_update(params, grad_shard, moment_one, moment_two)
     return (

time: 458 us -> 396 us (0.86)
  Pallas kernels: 217 us -> 269 us
  other arithmetic: 56.3 us -> 5.07 us
  matrix products: 54.8 us -> 14.4 us
  local copies, waits for them, and re-layouts: 41.1 us -> 13.6 us
  waiting for transfers between devices: 44.9 us -> 65.7 us
  starting transfers between devices: 13.5 us -> 2.16 us
    pallas_call x3 -> x8, Pallas kernels: 50.6 us -> 102 us  [the longest x7 75.9 us: stage(): pl.pallas_call(functools.partial(kernel, plan), out_shape=[jax.ShapeDtype...]
    reduce_sum x23 -> x0, other arithmetic: 26.6 us -> none  [the longest x4 10.5 us: depth_back(): jnp.sum(padded[:, offset:offset + length] * d_depth3, (0, 1))]
    dot_general x10 -> x2, matrix products: 27.6 us -> 5.88 us  [back_dot(): lax.dot_general(grad_in, weight, (((1,), (1,)), ((), ())), preferred_elem...]
    dot_general x10 -> x2, matrix products: 25.6 us -> 6.95 us  [forward_dot(): return jnp.dot(left_mat, weight, preferred_element_type=jnp.float32)]
    reduce_scatter x1, waiting for transfers between devices: 13.5 us -> 28 us  [seq_scatter(): return lax.psum_scatter(rows, SEQ, scatter_dimension=1, tiled=True)]
    slice x8 -> x0, local copies, waits for them, and re-layouts: 11.4 us -> none  [the longest x2 5.86 us: unpack(): piece = rows[first:first + -(-extent // LANES)]]
    ppermute x4 -> x0, starting transfers between devices: 11.3 us -> none  [the longest x2 6.29 us: with_halo(): before = lax.ppermute(last, axis, up)]
    add x4 -> x1, other arithmetic: 11.9 us -> 0.71 us  [attend_forward(): forward_dot(flat_all, weights['w_v']) + vector(weights, 'b_v')]
  transfers between devices with their start and end apart: 7 -> 3, of which waited for: 3 -> 2; matrix products, arithmetic and copies ran while one was open for 9% -> 2% of each run, Pallas kernels for 0% -> 0%
where the time goes in v1:
time: 396 us; the launch traced here: 389 us
  Pallas kernels  269 us (68%)
  waiting for transfers between devices  65.7 us (17%)
  between operations  19.5 us (5%)
  matrix products  14.4 us (4%)
  local copies, waits for them, and re-layouts  13.6 us (3%)
  other arithmetic  5.07 us (1%)
    pallas_call x7, Pallas kernels, stage(): pl.pallas_call(functools.partial(kernel, plan), out_shape=[jax.ShapeDtype...  75.9 us
    pallas_call x1, Pallas kernels, scatter(): pl.pallas_call(functools.partial(scatter_kernel, plan), out_shape=jax.Sha...  67.4 us
    pallas_call x1, Pallas kernels, gather(): pl.pallas_call(functools.partial(gather_kernel, plan), out_shape=jax.Shap...  63 us
    all_gather x1, waiting for transfers between devices, seq_gather(): lax.all_gather(rows.reshape(seq_count, -1, D), SEQ, axis=1, tiled=True)  37.6 us
    reduce_scatter x1, waiting for transfers between devices, seq_scatter(): return lax.psum_scatter(rows, SEQ, scatter_dimension=1, tiled=True)  28 us
    pallas_call x1, Pallas kernels, weight_grads(): pl.pallas_call(functools.partial(weight_kernel, plan, names, places), out...  26.3 us
    pallas_call x1, Pallas kernels, attend_back(): pl.pallas_call(attend_back_kernel, grid_spec=pltpu.PrefetchScalarGridSpec...  23.6 us
    pallas_call x1, Pallas kernels, attend(): pl.pallas_call(attend_kernel, grid_spec=pltpu.PrefetchScalarGridSpec(num_...  12.9 us
  transfers between devices with their start and end apart: 3, of which 2 were waited for; matrix products, arithmetic and copies ran while one was open for 2% of the time, Pallas kernels for 0%

profile of v1, /device:TPU:9, one launch (start us, length us, event | category | flops | bytes accessed | tf_op | source)
XLA Modules:
  0.0 389.4 jit_solution(6154239878035539765)
XLA Ops:
  7.9 1.9 collective-permute-start
  13.2 6.2 %concatenate.6 = bf16[200192]{0:T(1024)(128)(2,1)S(1)} concatenate(bf16[3584]{0:T(1024)(128)(2,1)S(1)} %broadcast_in_dim.4, f32[189368]{0:T(1024)} %param.12, bf16[4096]{0:T(1024)(128)(2,1)S(1)} %collective-permute-done, bf16[3144]{0:T(1024)(128)(2,1)S(1)} %broadcast_in_dim.5), dimensions={0} | concatenate | bytes 1179504 | tf_op jit(solution)/shard_map/concatenate | solution.py:111
  19.4 1.1 select_convert_fusion
  20.5 1.0 reshape.129.src
  21.5 63.0 %gather_params.1 = bf16[1486,8,512]{2,1,0:T(8,128)(2,1)} custom-call(bf16[47,8,512]{2,1,0:T(8,128)(2,1)} %reshape.129.src), custom_call_target="tpu_custom_call" | custom-call | tf_op jit(solution)/shard_map/gather_params/pallas_call | solution.py:317
  84.5 7.4 %ffn_first.1 = (f32[384,512]{1,0:T(8,128)}, bf16[384,512]{1,0:T(8,128)(2,1)}, bf16[384,512]{1,0:T(8,128)(2,1)}, bf16[4,512,512]{2,1,0:T(8,128)(2,1)}) custom-call(f32[384,512]{1,0:T(8,128)} %bitcast.67, bf16[11888,512]{1,0:T(8,128)(2,1)} %bitcast.44), custom_call_target="tpu_custom_call" | custom-call | tf_op jit(solution)/shard_map/ffn_first/pallas_call | solution.py:1099
  94.8 0.9 fusion.15.t_ref
  95.7 37.6 %all-gather.2.cloned.1.call-done = bf16[2,768,512]{2,1,0:T(8,128)(2,1)} async-done(((bf16[2,192,512]{2,1,0:T(8,128)(2,1)}), bf16[2,768,512]{2,1,0:T(8,128)(2,1)}) %all-gather.2.cloned.1.call-update) | async-done | bytes 1572880 | tf_op jit(solution)/shard_map/all_gather | solution.py:636
  133.3 3.8 convolution_convert_fusion
  137.1 3.2 fusion
  140.3 12.9 %attend.1 = (bf16[2,192,512]{2,1,0:T(8,128)(2,1)}, f32[2,192,128]{2,1,0:T(8,128)}) custom-call(s32[2]{0:T(128)} %len_ref.3, bf16[2,192,512]{2,1,0:T(8,128)(2,1)} %bitcast.74, bf16[2,768,512]{2,1,0:T(8,128)(2,1)} %bitcast.62, bf16[2,768,512]{2,1,0:T(8,128)(2,1)} %bitcast.64, f32[8,1024]{1,0:T(8,128)} %fusion.15.t_ref), custom_call_target="tpu_custom_call" | custom-call | tf_op jit(solution)/shard_map/attend/pallas_call | solution.py:576
  153.2 5.6 %gate.1 = (f32[384,512]{1,0:T(8,128)}, bf16[384,512]{1,0:T(8,128)(2,1)}, f32[384,1024]{1,0:T(8,128)}, f32[384,512]{1,0:T(8,128)}, bf16[2,512,512]{2,1,0:T(8,128)(2,1)}) custom-call(bf16[384,512]{1,0:T(8,128)(2,1)} %bitcast.69, f32[384,512]{1,0:T(8,128)} %get-tuple-element.53.x.x_one, f32[384,1]{1,0:T(8,128)} %reshape.151.valid, bf16[11888,512]{1,0:T(8,128)(2,1)} %bitcast.47), custom_call_target="tpu_custom_call" | custom-call | tf_op jit(solution)/shard_map/gate/pallas_call | solution.py:1099
  158.7 19.1 %depth.1 = (f32[384,512]{1,0:T(8,128)}, f32[8,512]{1,0:T(8,128)}, f32[2,224,512]{2,1,0:T(8,128)}) custom-call(f32[384,512]{1,0:T(8,128)} %get-tuple-element.55.u, f32[384,1]{1,0:T(8,128)} %reshape.151.valid, bf16[11888,512]{1,0:T(8,128)(2,1)} %bitcast.48), custom_call_target="tpu_custom_call" | custom-call | tf_op jit(solution)/shard_map/depth/pallas_call | solution.py:1099
  177.8 11.8 %middle.1 = (f32[384,512]{1,0:T(8,128)}, f32[384,512]{1,0:T(8,128)}, f32[384,512]{1,0:T(8,128)}, f32[8,512]{1,0:T(8,128)}, f32[8,512]{1,0:T(8,128)}, /*index=5*/...) custom-call(f32[384,512]{1,0:T(8,128)} %get-tuple-element.54.x, ...), custom_call_target="tpu_custom_call" | custom-call | tf_op jit(solution)/shard_map/middle/pallas_call | solution.py:1099
  189.6 17.6 %depth_back.1 = (f32[384,512]{1,0:T(8,128)}, f32[32,512]{1,0:T(8,128)}) custom-call(f32[384,512]{1,0:T(8,128)} %get-tuple-element.59.dz, f32[384,512]{1,0:T(8,128)} %get-tuple-element.56.depth, f32[8,512]{1,0:T(8,128)} %get-tuple-element.60.stats, f32[8,512]{1,0:T(8,128)} %get-tuple-element.61.local, f32[384,1]{1,0:T(8,128)} %reshape.151.valid, ...), custom_call_target="tpu_custom_call" | custom-call | tf_op jit(solution)/shard_map/depth_back/pallas_call | solution.py:1099
  207.2 5.1 %gate_back.1 = (bf16[384,1024]{1,0:T(8,128)(2,1)}, f32[384,512]{1,0:T(8,128)}, bf16[384,512]{1,0:T(8,128)(2,1)}, bf16[384,512]{1,0:T(8,128)(2,1)}, f32[8,512]{1,0:T(8,128)}) custom-call(f32[384,512]{1,0:T(8,128)} %get-tuple-element.63.du, f32[384,1024]{1,0:T(8,128)} %get-tuple-element.64.pre_gate, f32[384,512]{1,0:T(8,128)} %get-tuple-element.54.x, ...), custom_call_target="tpu_custom_call" | custom-call | tf_op jit(solution)/shard_map/gate_back/pallas_call | solution.py:1099
  212.3 23.6 %attend_back.1 = (bf16[2,192,512]{2,1,0:T(8,128)(2,1)}, bf16[2,768,512]{2,1,0:T(8,128)(2,1)}, bf16[2,768,512]{2,1,0:T(8,128)(2,1)}, f32[8,1024]{1,0:T(8,128)}, f32[8,512]{1,0:T(8,128)}) custom-call(s32[2]{0:T(128)} %len_ref.3, bf16[2,192,512]{2,1,0:T(8,128)(2,1)} %bitcast.75, bf16[2,768,512]{2,1,0:T(8,128)(2,1)} %bitcast.63, bf16[2,768,512]{2,1,0:T(8,128)(2,1)} %bitcast.65, ...), custom_call_target="tpu_custom_call" | custom-call | tf_op jit(solution)/shard_map/attend_back/pallas_call | solution.py:603
  235.8 2.6 fusion.5
  238.5 3.2 fusion.1
  246.7 28.0 %reduce-scatter.2.cloned.1.call-done = bf16[2,192,512]{2,1,0:T(8,128)(2,1)} async-done(((bf16[2,768,512]{2,1,0:T(8,128)(2,1)}), bf16[2,192,512]{2,1,0:T(8,128)(2,1)}) %reduce-scatter.2.cloned.1.call-update) | async-done | bytes 393232 | tf_op jit(solution)/shard_map/reduce_scatter | solution.py:640
  274.7 9.4 %ffn_first_back.1 = (f32[384,512]{1,0:T(8,128)}, bf16[384,2048]{1,0:T(8,128)(2,1)}, bf16[384,512]{1,0:T(8,128)(2,1)}, bf16[384,512]{1,0:T(8,128)(2,1)}, bf16[384,2048]{1,0:T(8,128)(2,1)}, /*index=5*/f32[16,512]{1,0:T(8,128)}) custom-call(f32[384,512]{1,0:T(8,128)} %bitcast.68, f32[384,512]{1,0:T(8,128)} %get-tuple-element.53.x.x_one, ...), custom_call_target="tpu_custom_call" | custom-call | tf_op jit(solution)/shard_map/ffn_first_back/pallas_call | solution.py:1099
  284.1 26.3 %weight_grads.1.g = bf16[1487,8,512]{2,1,0:T(8,128)(2,1)} custom-call(bf16[1536,512]{1,0:T(8,128)(2,1)} %bitcast.57, bf16[1536,512]{1,0:T(8,128)(2,1)} %bitcast.54, bf16[1536,512]{1,0:T(8,128)(2,1)} %bitcast.58, bf16[1536,512]{1,0:T(8,128)(2,1)} %bitcast.60, bf16[384,512]{1,0:T(8,128)(2,1)} %get-tuple-element.75.refs_4_, ...), custom_call_target="tpu_custom_call" | custom-call | tf_op jit(solution)/shard_map/weight_grads/pallas_call | solution.py:483
  310.4 67.4 %scatter_grads.1 = f32[48,8,512]{2,1,0:T(8,128)S(1)} custom-call(bf16[1487,8,512]{2,1,0:T(8,128)(2,1)} %weight_grads.1.g), custom_call_target="tpu_custom_call" | custom-call | tf_op jit(solution)/shard_map/scatter_grads/pallas_call | solution.py:433
  379.2 3.1 multiply_subtract_fusion
  (37 shorter events, 8.0 us)
Async XLA Ops:
  7.2 126.1 %all-gather.2.cloned.1.call-start = ((), (), s32[]{:S(2)}) async-start(), calls=%async_computation.1 | async-start | bytes 1966080 | tf_op jit(solution)/shard_map/all_gather | solution.py:636
  7.9 5.2 %collective-permute-start = (bf16[4096]{0:T(1024)(128)(2,1)S(1)}, bf16[4096]{0:T(1024)(128)(2,1)S(1)}, u32[]{:S(2)}, u32[]{:S(2)}) collective-permute-start(bf16[4096]{0:T(1024)(128)(2,1)S(1)} %slice.50), channel_id=1, source_target_pairs={{1,0},{2,1},{3,2},{4,3},{5,4},{6,5},{7,6},{8,7},{9,8},{10,9},{11,1... | collective-permute-start | bytes 24584 | tf_op jit(solution)/shard_map/ppermute | solution.py:107
  84.5 7.7 %copy-start.6 = (s32[2]{0:T(128)S(1)}, s32[2]{0:T(128)}, u32[]{:S(2)}) copy-start(s32[2]{0:T(128)} %len_ref.3) | copy-start | bytes 28
  84.5 8.7 %copy-start.5 = (s32[1535]{0:T(1024)S(1)}, s32[1535]{0:T(1024)}, u32[]{:S(2)}) copy-start(s32[1535]{0:T(1024)} %param.11) | copy-start | bytes 18424
  92.0 182.8 %reduce-scatter.2.cloned.1.call-start = ((), (), s32[]{:S(2)}) async-start(), calls=%async_computation.2 | async-start | bytes 1966080 | tf_op jit(solution)/shard_map/reduce_scatter | solution.py:640
  133.3 3.8 copy-start
  235.8 2.7 copy-start.1
  241.7 3.8 copy-start.7
  310.4 67.7 %copy-start.4 = (f32[189368]{0:T(1024)S(1)}, f32[189368]{0:T(1024)}, u32[]{:S(2)}) copy-start(f32[189368]{0:T(1024)} %param.14) | copy-start | bytes 2272420
  377.9 1.1 copy-start.2
  377.9 1.3 copy-start.3
Sparse Core Ops, SparseCore 0:
  92.1 41.1 all-gather.1
  241.9 32.8 reduce-scatter.1
